TPU v7x, 256 devices: a whole 4x4x8 slice. The times are simulated.
256 devices in a mesh: rep: 2 (over core), dp: 128 (over x, y, z).
Axes of the slice: x: 4, y: 4, z: 8, core: 2. Of those that a mesh axis runs over, the one named last changes fastest.
Arguments:
- x: bfloat16 [256, 2048, 512], P(('rep', 'dp')), parts along dimension 0
- dy: bfloat16 [256, 2048, 512], P(('rep', 'dp')), parts along dimension 0
- w_gate: bfloat16 [2, 512, 2048], replicated
- w_up: bfloat16 [2, 512, 2048], replicated
- w_down: bfloat16 [2, 2048, 512], replicated
- m_w_gate: float32 [2, 512, 2048], replicated
- m_w_up: float32 [2, 512, 2048], replicated
- m_w_down: float32 [2, 2048, 512], replicated
- v_w_gate: float32 [2, 512, 2048], replicated
- v_w_up: float32 [2, 512, 2048], replicated
- v_w_down: float32 [2, 2048, 512], replicated
Outputs:
- output 1: bfloat16 [4, 512, 2048], P('rep'), parts along dimension 0
- output 2: bfloat16 [4, 512, 2048], P('rep'), parts along dimension 0
- output 3: bfloat16 [4, 2048, 512], P('rep'), parts along dimension 0
- output 4: float32 [4, 512, 2048], P('rep'), parts along dimension 0
- output 5: float32 [4, 512, 2048], P('rep'), parts along dimension 0
- output 6: float32 [4, 2048, 512], P('rep'), parts along dimension 0
- output 7: float32 [4, 512, 2048], P('rep'), parts along dimension 0
- output 8: float32 [4, 512, 2048], P('rep'), parts along dimension 0
- output 9: float32 [4, 2048, 512], P('rep'), parts along dimension 0
There are 2 independent parts. A program takes and returns all parts, laid end to end along the dimension named above; an argument that names none is the same for every part.
All inputs are finite; a program needn't handle non-finite values.
Results may differ from a plain program's by a relative error of at most 0.022.
Values are sent between devices in bfloat16 or wider.
A program may use at most 768 MiB of HBM per device.

v0:
```python
import jax
import jax.numpy as jnp
from jax import lax
from jax.sharding import PartitionSpec as P

NAMES = ("w_gate", "w_up", "w_down")


def matmul(a, w):
    return jnp.dot(a, w, preferred_element_type=jnp.float32).astype(jnp.bfloat16)


def normed(h):
    wide = h.astype(jnp.float32)
    scale = lax.rsqrt(jnp.mean(wide**2, -1, keepdims=True) + 1e-6)
    return (wide * scale).astype(jnp.bfloat16)


def layer(h, w):
    a = normed(h)
    gate = jnp.dot(a, w["w_gate"], preferred_element_type=jnp.float32)
    up = jnp.dot(a, w["w_up"], preferred_element_type=jnp.float32)
    return h + matmul((jax.nn.silu(gate) * up).astype(jnp.bfloat16), w["w_down"])


def adamw(w, m, v, g):
    m = 0.9 * m + 0.1 * g
    v = 0.95 * v + 0.05 * g * g
    step = m * lax.rsqrt(v + 1e-8) + 0.1 * w
    return (w - 0.02 * step).astype(jnp.bfloat16), m, v


def clipped(gradients, sum_of_squares, count):
    factor = jnp.minimum(1.0, 0.5 * lax.rsqrt(sum_of_squares / count + 1e-30))
    return [g * factor for g in gradients]


def solution(mesh):
    def step(x, dy, *arrays):
        weights, m, v = (arrays[i : i + 3] for i in (0, 3, 6))
        layers = weights[0].shape[0]
        h, kept = x[0], []
        for number in range(layers):
            kept.append(h)
            h = layer(h, {name: w[number] for name, w in zip(NAMES, weights, strict=True)})
        by_h, summed = dy[0], [None] * layers
        for number in reversed(range(layers)):
            _, back = jax.vjp(lambda w, h: layer(h, w), {name: w[number] for name, w in zip(NAMES, weights, strict=True)}, kept[number])
            by_w, by_h = back(by_h)
            summed[number] = [lax.psum(by_w[name], "dp") for name in NAMES]
        gradients = [jnp.stack([summed[number][i] for number in range(layers)]).astype(jnp.float32) for i in range(3)]
        gradients = clipped(gradients, sum(jnp.sum(g * g) for g in gradients), sum(g.size for g in gradients))
        new = [adamw(w.astype(jnp.float32), m, v, g) for w, m, v, g in zip(weights, m, v, gradients, strict=True)]
        return tuple(one[which] for which in range(3) for one in new)

    return jax.shard_map(
        step,
        mesh=mesh,
        in_specs=(P(("rep", "dp"), None, None),) * 2 + (P(None, None, None),) * 9,
        out_specs=(P("rep", None, None),) * 9,
        check_vma=False,
    )
```

profile of v0, /device:TPU:2, one launch (start us, length us, event | category | flops | bytes accessed | tf_op | source)
XLA Modules:
  0.0 578.3 jit_solution(11668856283066067141)
XLA Ops:
  7.2 0.0 all-reduce.3.cloned.1.call-start
  7.2 2.9 copy.20
  10.2 0.0 copy-start.5
  10.2 0.5 fusion.36
  10.6 0.0 copy-start.19
  10.6 4.2 copy.21
  14.8 0.0 copy-start.13
  14.8 10.3 %convolution_convert_fusion.1 = bf16[2048,2048]{1,0:T(8,128)(2,1)} fusion(bf16[1,2048,512]{2,1,0:T(8,128)(2,1)} %param.12, bf16[2,2048,512]{2,1,0:T(8,128)(2,1)} %param.15), kind=kOutput, calls=%fused_computation.61 | convolution fusion | flops 4299161600 | bytes 12582912 | tf_op jit(solution)/shard_map/transpose(jvp())/dot_general | solution.py:10
  25.1 0.0 copy-done.9
  25.1 0.0 copy-done.13
  25.1 8.2 %fusion.76 = f32[2048,2048]{1,0:T(8,128)} fusion(bf16[2,512,2048]{2,1,0:T(8,128)(2,1)S(1)} %copy-done.9, bf16[1,2048,512]{2,1,0:T(8,128)(2,1)S(1)} %copy-done.13, f32[2048]{0:T(1024)S(1)} %add_rsqrt_fusion), kind=kOutput, calls=%fused_computation.112 | convolution fusion | flops 4298113024 | bytes 20979712 | tf_op jit(solution)/shard_map/dot_general | solution.py:21
  33.4 0.0 copy-done.19
  33.4 17.4 %multiply_convert_fusion.1 = (bf16[2048,2048]{1,0:T(8,128)(2,1)}, f32[2048,2048]{1,0:T(8,128)}) fusion(f32[2048,2048]{1,0:T(8,128)} %fusion.76, bf16[2,512,2048]{2,1,0:T(8,128)(2,1)} %param.14, bf16[1,2048,512]{2,1,0:T(8,128)(2,1)S(1)} %copy-done.13, f32[2048]{0:T(1024)S(1)} %add_rsqrt_fusion), kind=kOutput, calls=%fused_computation.17 | convolution fusion | flops 4323278848 | bytes 46145536 | tf_op jit(solution)/shard_map/dot_general | solution.py:22
  50.8 0.0 copy-done.5
  50.8 0.0 copy-start.11
  50.8 9.1 %fusion.40 = (f32[2048]{0:T(1024)S(1)}, bf16[2048,512]{0,1:T(8,128)(2,1)S(1)}) fusion(bf16[2048,2048]{1,0:T(8,128)(2,1)} %get-tuple-element.24, bf16[2,2048,512]{2,1,0:T(8,128)(2,1)} %param.15, bf16[1,2048,512]{1,2,0:T(8,128)(2,1)S(1)} %copy.20), kind=kOutput, calls=%fused_computation.73 | convolution fusion | flops 4300208128 | bytes 14688256 | tf_op jit(solution)/shard_map/dot_general | solution.py:10
  59.9 0.0 copy-start.15
  59.9 0.0 copy-start.17
  59.9 1.3 copy-done.15
  61.2 0.0 copy-done.17
  61.2 0.0 copy-done.11
  61.2 8.2 %fusion.65 = f32[2048,2048]{1,0:T(8,128)} fusion(bf16[2,512,2048]{2,1,0:T(8,128)(2,1)S(1)} %copy-done.11, bf16[2048,512]{0,1:T(8,128)(2,1)S(1)} %get-tuple-element.27, f32[2048]{0:T(1024)S(1)} %fusion.95), kind=kOutput, calls=%fused_computation.101 | convolution fusion | flops 4298113024 | bytes 20979712 | tf_op jit(solution)/shard_map/jvp()/dot_general | solution.py:22
  69.4 0.0 copy-start.14
  69.4 23.2 %fusion.2 = (bf16[2048,2048]{1,0:T(8,128)(2,1)}, f32[2048,2048]{1,0:T(8,128)}) fusion(f32[2048,2048]{1,0:T(8,128)} %fusion.65, bf16[2048,2048]{1,0:T(8,128)(2,1)} %convolution_convert_fusion.1, bf16[2,512,2048]{2,1,0:T(8,128)(2,1)} %param.13, bf16[2048,512]{0,1:T(8,128)(2,1)} %copy-done.15, f32[2048]{0:T(1024)S(1)} %fusion.95), kind=kOutput, calls=%fused_computation.8 | convolution fusion | flops 4348444672 | bytes 54534144 | tf_op jit(solution)/shard_map/jvp()/dot_general | solution.py:21
  92.7 0.0 copy-done.14
  92.7 0.0 copy-start.16
  92.7 14.5 %fusion.55 = bf16[1,2048,512]{2,1,0:T(8,128)(2,1)} fusion(f32[2048,2048]{1,0:T(8,128)} %fusion.65, bf16[1,2048,512]{2,1,0:T(8,128)(2,1)S(1)} %copy-done.14, f32[2048,2048]{1,0:T(8,128)} %get-tuple-element.29), kind=kOutput, calls=%fused_computation.93 | convolution fusion | flops 4321181696 | bytes 37748736 | tf_op jit(solution)/shard_map/transpose(jvp())/dot_general | solution.py:10
  107.1 0.0 copy-done.16
  107.2 0.0 copy-start.12
  107.2 12.4 %fusion.54 = bf16[1,512,2048]{2,1,0:T(8,128)(2,1)} fusion(bf16[2048,2048]{1,0:T(8,128)(2,1)} %convolution_convert_fusion.1, bf16[2048,512]{0,1:T(8,128)(2,1)S(1)} %copy-done.16, f32[2048]{0:T(1024)S(1)} %fusion.95, f32[2048,2048]{1,0:T(8,128)} %get-tuple-element.29), kind=kOutput, calls=%fused_computation.92 | convolution fusion | flops 4324327424 | bytes 29368320 | tf_op jit(solution)/shard_map/transpose(jvp())/dot_general | solution.py:22
  119.5 0.0 copy-done.12
  119.5 11.3 %fusion.47 = bf16[2048,512]{0,1:T(8,128)(2,1)S(1)} fusion(bf16[2048,2048]{1,0:T(8,128)(2,1)} %convolution_convert_fusion.1, bf16[2,512,2048]{2,1,0:T(8,128)(2,1)S(1)} %copy-done.12, f32[2048,2048]{1,0:T(8,128)} %get-tuple-element.29), kind=kOutput, calls=%fused_computation.84 | convolution fusion | flops 4321181696 | bytes 29360128 | tf_op jit(solution)/shard_map/transpose(jvp())/dot_general | solution.py:22
  130.9 0.0 copy-start.10
  130.9 9.3 %fusion.52 = bf16[1,512,2048]{2,1,0:T(8,128)(2,1)} fusion(bf16[2048,2048]{1,0:T(8,128)(2,1)} %get-tuple-element.28, bf16[2048,512]{0,1:T(8,128)(2,1)S(1)} %copy-done.16, f32[2048]{0:T(1024)S(1)} %fusion.95), kind=kOutput, calls=%fused_computation.90 | convolution fusion | flops 4298113024 | bytes 12591104 | tf_op jit(solution)/shard_map/transpose(jvp())/dot_general | solution.py:21
  140.1 0.0 copy-done.10
  140.2 9.0 %fusion.42 = (f32[2048]{0:T(1024)S(1)}, bf16[2048,512]{0,1:T(8,128)(2,1)S(1)}) fusion(bf16[2048,512]{0,1:T(8,128)(2,1)S(1)} %copy-done.16, bf16[2048,512]{0,1:T(8,128)(2,1)S(1)} %fusion.47, bf16[2048,2048]{1,0:T(8,128)(2,1)} %get-tuple-element.28, bf16[2,512,2048]{2,1,0:T(8,128)(2,1)S(1)} %copy-done.10), kind=kOutput, calls=%fused_computation.75 | convolution fusion | flops 4300208128 | bytes 16785408 | tf_op jit(solution)/shard_map/transpose(jvp())/dot_general | solution.py:21
  149.2 0.0 copy-done.18
  149.2 0.0 copy-done.7
  149.2 1.4 fusion.62
  150.6 0.0 copy-start.8
  150.6 9.7 %fusion.51 = bf16[1,2048,512]{2,1,0:T(8,128)(2,1)} fusion(bf16[2048,2048]{1,0:T(8,128)(2,1)} %get-tuple-element.24, bf16[2048,512]{0,1:T(8,128)(2,1)S(1)} %fusion.62), kind=kOutput, calls=%fused_computation.89 | convolution fusion | flops 4296015872 | bytes 12582912 | tf_op jit(solution)/shard_map/transpose(jvp())/dot_general | solution.py:10
  160.3 0.0 copy-done.8
  160.3 5.1 convolution_convert_fusion
  165.4 0.0 copy-done.6
  165.4 0.0 copy-done.20
  165.4 0.0 copy-start.21
  165.4 13.5 %fusion.53 = bf16[1,512,2048]{2,1,0:T(8,128)(2,1)} fusion(bf16[2048,2048]{1,0:T(8,128)(2,1)S(1)} %convolution_convert_fusion, f32[2048,2048]{1,0:T(8,128)} %fusion.76, bf16[1,2048,512]{1,2,0:T(8,128)(2,1)S(1)} %copy-done.6, f32[2048]{0:T(1024)S(1)} %copy-done.20), kind=kOutput, calls=%fused_computation.91 | convolution fusion | flops 4324327424 | bytes 29368320 | tf_op jit(solution)/shard_map/transpose(jvp())/dot_general | solution.py:22
  178.9 0.0 copy-done.21
  178.9 17.6 %fusion.56 = bf16[1,512,2048]{2,1,0:T(8,128)(2,1)} fusion(f32[2048,2048]{1,0:T(8,128)} %fusion.76, f32[2048,2048]{1,0:T(8,128)} %get-tuple-element.25, bf16[2048,2048]{1,0:T(8,128)(2,1)} %copy-done.21, bf16[1,2048,512]{1,2,0:T(8,128)(2,1)S(1)} %copy-done.6, f32[2048]{0:T(1024)S(1)} %copy-done.20), kind=kOutput, calls=%fused_computation.94 | convolution fusion | flops 4345298944 | bytes 46145536 | tf_op jit(solution)/shard_map/transpose(jvp())/dot_general | solution.py:21
  196.5 0.0 all-reduce.3.cloned.1.call-update
  196.5 317.7 %all-reduce.3.cloned.1.call-done = (bf16[1,512,2048]{2,1,0:T(8,128)(2,1)}, bf16[1,512,2048]{2,1,0:T(8,128)(2,1)}, bf16[1,512,2048]{2,1,0:T(8,128)(2,1)}, bf16[1,...) async-done(((bf16[1,512,2048]{2,1,0:T(8,128)(2,1)}, bf16[1,512,2048]{2,1,0:T(8,128)(2,1)}, bf16[1,512,2048]{2,1,0:T(8,128)(2,1)}, ...) | async-done | bytes 12582928 | tf_op jit(solution)/shard_map/psum | solution.py:50
  514.2 4.5 fusion.24
  518.7 4.3 fusion.23
  523.0 0.0 copy-done
  523.0 0.0 copy-done.1
  523.0 2.8 fusion.22
  527.7 0.0 copy-start.2
  527.7 0.0 copy-start.3
  527.8 0.0 copy-start.4
  527.8 15.8 %fusion.30 = (bf16[2,2048,512]{2,1,0:T(8,128)(2,1)}, f32[2,2048,512]{2,1,0:T(8,128)}, f32[2,2048,512]{2,1,0:T(8,128)}) fusion(bf16[2,2048,512]{2,1,0:T(8,128)(2,1)} %param.15, f32[]{:T(128)S(6)} %min_shard_map.3, bf16[1,2048,512]{2,1,0:T(8,128)(2,1)} %get-tuple-element.13, bf16[1,2048,512]{2,1,0:T(8,128)(2,1)} %get-tuple-element.14, ...), kind=kLoop, calls=%fused_computation.54 | loop fusion | flops 41943040 | bytes 46137348 | tf_op jit(solution)/shard_map/convert_element_type | solution.py:30
  543.6 0.0 copy-done.2
  543.6 0.0 copy-done.3
  543.6 0.0 copy-done.4
  543.6 27.4 %fusion.21 = (bf16[2,512,2048]{2,1,0:T(8,128)(2,1)}, f32[2,512,2048]{2,1,0:T(8,128)}, f32[2,512,2048]{2,1,0:T(8,128)}, bf16[2,512,2048]{2,1,0:T(8,128)(2,1)}, f3...) fusion(bf16[2,512,2048]{2,1,0:T(8,128)(2,1)} %param.13, f32[]{:T(128)S(6)} %min_shard_map.3, ...), kind=kLoop, calls=%fused_computation.45 | loop fusion | flops 83886080 | bytes 92274688 | tf_op jit(solution)/shard_map/convert_element_type | solution.py:30
  (10 shorter events, 0.0 us)
Async XLA Ops:
  7.2 507.0 %all-reduce.3.cloned.1.call-start = ((), (), s32[]{:S(2)}) async-start(), calls=%async_computation | async-start | bytes 25165824 | tf_op jit(solution)/shard_map/psum | solution.py:50
  10.2 40.6 %copy-start.5 = (bf16[1,2048,512]{1,2,0:T(8,128)(2,1)}, bf16[1,2048,512]{1,2,0:T(8,128)(2,1)S(1)}, u32[]{:S(2)}) copy-start(bf16[1,2048,512]{1,2,0:T(8,128)(2,1)S(1)} %copy.20) | copy-start | bytes 6291460
  10.6 22.7 %copy-start.19 = (f32[2048]{0:T(1024)}, f32[2048]{0:T(1024)S(1)}, u32[]{:S(2)}) copy-start(f32[2048]{0:T(1024)S(1)} %add_rsqrt_fusion) | copy-start | bytes 24580
  14.8 10.3 %copy-start.9 = (bf16[2,512,2048]{2,1,0:T(8,128)(2,1)S(1)}, bf16[2,512,2048]{2,1,0:T(8,128)(2,1)}, u32[]{:S(2)}) copy-start(bf16[2,512,2048]{2,1,0:T(8,128)(2,1)} %param.13) | copy-start | bytes 12582916
  14.8 10.3 %copy-start.13 = (bf16[1,2048,512]{2,1,0:T(8,128)(2,1)S(1)}, bf16[1,2048,512]{2,1,0:T(8,128)(2,1)}, u32[]{:S(2)}) copy-start(bf16[1,2048,512]{2,1,0:T(8,128)(2,1)} %param.11) | copy-start | bytes 6291460
  50.8 10.4 %copy-start.11 = (bf16[2,512,2048]{2,1,0:T(8,128)(2,1)S(1)}, bf16[2,512,2048]{2,1,0:T(8,128)(2,1)}, u32[]{:S(2)}) copy-start(bf16[2,512,2048]{2,1,0:T(8,128)(2,1)} %param.14) | copy-start | bytes 12582916
  59.9 1.3 copy-start.15
  59.9 1.3 copy-start.17
  69.4 23.3 %copy-start.14 = (bf16[1,2048,512]{2,1,0:T(8,128)(2,1)S(1)}, bf16[1,2048,512]{2,1,0:T(8,128)(2,1)}, u32[]{:S(2)}) copy-start(bf16[1,2048,512]{2,1,0:T(8,128)(2,1)} %param.12) | copy-start | bytes 6291460
  92.7 14.5 %copy-start.16 = (bf16[2048,512]{0,1:T(8,128)(2,1)S(1)}, bf16[2048,512]{0,1:T(8,128)(2,1)}, u32[]{:S(2)}) copy-start(bf16[2048,512]{0,1:T(8,128)(2,1)} %copy-done.15) | copy-start | bytes 6291460
  107.2 12.4 %copy-start.12 = (bf16[2,512,2048]{2,1,0:T(8,128)(2,1)S(1)}, bf16[2,512,2048]{2,1,0:T(8,128)(2,1)}, u32[]{:S(2)}) copy-start(bf16[2,512,2048]{2,1,0:T(8,128)(2,1)} %param.14) | copy-start | bytes 12582916
  130.9 9.3 %copy-start.10 = (bf16[2,512,2048]{2,1,0:T(8,128)(2,1)S(1)}, bf16[2,512,2048]{2,1,0:T(8,128)(2,1)}, u32[]{:S(2)}) copy-start(bf16[2,512,2048]{2,1,0:T(8,128)(2,1)} %param.13) | copy-start | bytes 12582916
  140.1 9.0 %copy-start.18 = (f32[2048]{0:T(1024)S(1)}, f32[2048]{0:T(1024)}, u32[]{:S(2)}) copy-start(f32[2048]{0:T(1024)} %copy-done.17) | copy-start | bytes 24580
  140.2 9.1 %copy-start.7 = (bf16[1,2048,512]{1,2,0:T(8,128)(2,1)S(1)}, bf16[1,2048,512]{1,2,0:T(8,128)(2,1)}, u32[]{:S(2)}) copy-start(bf16[1,2048,512]{1,2,0:T(8,128)(2,1)} %copy.21) | copy-start | bytes 6291460
  150.6 9.7 %copy-start.8 = (bf16[2,2048,512]{2,1,0:T(8,128)(2,1)S(1)}, bf16[2,2048,512]{2,1,0:T(8,128)(2,1)}, u32[]{:S(2)}) copy-start(bf16[2,2048,512]{2,1,0:T(8,128)(2,1)} %param.15) | copy-start | bytes 12582916
  160.3 5.1 copy-start.6
  160.3 5.1 copy-start.20
  165.4 13.5 %copy-start.21 = (bf16[2048,2048]{1,0:T(8,128)(2,1)}, bf16[2048,2048]{1,0:T(8,128)(2,1)S(1)}, u32[]{:S(2)}) copy-start(bf16[2048,2048]{1,0:T(8,128)(2,1)S(1)} %convolution_convert_fusion) | copy-start | bytes 25165828
  514.2 8.8 %copy-start = (bf16[1,512,2048]{2,1,0:T(8,128)(2,1)S(1)}, bf16[1,512,2048]{2,1,0:T(8,128)(2,1)}, u32[]{:S(2)}) copy-start(bf16[1,512,2048]{2,1,0:T(8,128)(2,1)} %get-tuple-element.9) | copy-start | bytes 6291460
  514.2 8.8 %copy-start.1 = (bf16[1,512,2048]{2,1,0:T(8,128)(2,1)S(1)}, bf16[1,512,2048]{2,1,0:T(8,128)(2,1)}, u32[]{:S(2)}) copy-start(bf16[1,512,2048]{2,1,0:T(8,128)(2,1)} %get-tuple-element.10) | copy-start | bytes 6291460
  527.7 15.9 %copy-start.2 = (bf16[1,512,2048]{2,1,0:T(8,128)(2,1)S(1)}, bf16[1,512,2048]{2,1,0:T(8,128)(2,1)}, u32[]{:S(2)}) copy-start(bf16[1,512,2048]{2,1,0:T(8,128)(2,1)} %get-tuple-element.10) | copy-start | bytes 6291460
  527.7 15.9 %copy-start.3 = (bf16[1,512,2048]{2,1,0:T(8,128)(2,1)S(1)}, bf16[1,512,2048]{2,1,0:T(8,128)(2,1)}, u32[]{:S(2)}) copy-start(bf16[1,512,2048]{2,1,0:T(8,128)(2,1)} %get-tuple-element.11) | copy-start | bytes 6291460
  527.8 15.9 %copy-start.4 = (bf16[1,512,2048]{2,1,0:T(8,128)(2,1)S(1)}, bf16[1,512,2048]{2,1,0:T(8,128)(2,1)}, u32[]{:S(2)}) copy-start(bf16[1,512,2048]{2,1,0:T(8,128)(2,1)} %get-tuple-element.12) | copy-start | bytes 6291460
Sparse Core Ops, SparseCore 0:
  196.7 317.4 all-reduce.2
where the time goes:
time: 585 us; the launch traced here: 578 us
  waiting for transfers between devices  318 us (54%)
  matrix products  179 us (31%)
  other arithmetic  56.6 us (10%)
  between operations  16.7 us (3%)
  local copies, waits for them, and re-layouts  8.48 us (1%)
    psum x1, waiting for transfers between devices, step(): summed[number] = [lax.psum(by_w[name], 'dp') for name in NAMES]  318 us
    dot_general x5, matrix products, layer(): gate = jnp.dot(a, w['w_gate'], preferred_element_type=jnp.float32)  67.3 us
    dot_general x5, matrix products, layer(): up = jnp.dot(a, w['w_up'], preferred_element_type=jnp.float32)  62.8 us
    dot_general x5, matrix products, matmul(): jnp.dot(a, w, preferred_element_type=jnp.float32).astype(jnp.bfloat16)  48.6 us
    convert_element_type x2, other arithmetic, adamw(): return ((w - 0.02 * step).astype(jnp.bfloat16), m, v)  43.2 us
  transfers between devices with their start and end apart: 1, of which 1 were waited for; matrix products, arithmetic and copies ran while one was open for 0% of the time, Pallas kernels for 0%

commit v1 on v0

v1 whole, which is shorter than its diff:
```python
import functools
import heapq

import jax
import jax.numpy as jnp
from jax import lax
from jax.experimental import pallas as pl
from jax.experimental.pallas import tpu as pltpu
from jax.sharding import PartitionSpec as P

NAMES = ("w_gate", "w_up", "w_down")
SIZES = {"x": 4, "y": 4, "z": 8}
LANES = 512
MESH = pl.DeviceIdType.MESH
ORDERS = (("x", "y", "z"), ("y", "z", "x"), ("z", "x", "y"))


def matmul(a, w):
    return jnp.dot(a, w, preferred_element_type=jnp.float32).astype(jnp.bfloat16)


def normed(h):
    wide = h.astype(jnp.float32)
    scale = lax.rsqrt(jnp.mean(wide**2, -1, keepdims=True) + 1e-6)
    return (wide * scale).astype(jnp.bfloat16)


def layer(h, w):
    a = normed(h)
    gate = jnp.dot(a, w["w_gate"], preferred_element_type=jnp.float32)
    up = jnp.dot(a, w["w_up"], preferred_element_type=jnp.float32)
    return h + matmul((jax.nn.silu(gate) * up).astype(jnp.bfloat16), w["w_down"])


def position():
    dp = lax.axis_index("dp")
    ny, nz = SIZES["y"], SIZES["z"]
    return {"x": dp // (ny * nz), "y": (dp // nz) % ny, "z": dp % nz}


def along(me, axis, delta):
    at = dict(me)
    at[axis] = (me[axis] + delta + SIZES[axis]) % SIZES[axis]
    return {"dp": (at["x"] * SIZES["y"] + at["y"]) * SIZES["z"] + at["z"]}


def meet(me):
    barrier = pltpu.get_barrier_semaphore()
    count = 0
    for axis, n in SIZES.items():
        for delta in range(1, n):
            pl.semaphore_signal(barrier, inc=1, device_id=along(me, axis, delta), device_id_type=MESH)
            count += 1
    pl.semaphore_wait(barrier, count)


def cut(axes, axis, i, wide):
    lead = (slice(None),) * axes.index(axis)
    if wide and axis == "z":
        return lead + (i // 4, slice(None), pl.ds(pl.multiple_of((i % 4) * LANES, LANES), LANES))
    return lead + (i,)


def shape_of(axes, wide):
    if wide and "z" in axes:
        return tuple(SIZES[a] for a in axes if a != "z") + (SIZES["z"] // 4, 16, 4 * LANES)
    return tuple(SIZES[a] for a in axes) + (16, LANES)


def at(index, lead):
    out, rest = [], list(lead)
    for part in index:
        out.append(rest.pop(0) if isinstance(part, slice) and rest else part)
    return tuple(out[: len(index)]) + tuple(rest)


def add_into(slot, local, index):
    shape = slot.shape[:-2]
    total = 1
    for n in shape:
        total *= n

    def body(i, _):
        lead, rest = [], i
        for n in reversed(shape):
            lead.insert(0, rest % n)
            rest = rest // n
        term = local[at(index, lead)].astype(jnp.float32)
        slot[tuple(lead)] = (slot[tuple(lead)].astype(jnp.float32) + term).astype(slot.dtype)
        return 0

    lax.fori_loop(0, total, body, 0, unroll=False)


def reduce_one(me, number, wide, order, sign, grad, slots, sends, recvs, out, drain):
    axes, local, copy_number, near = ("x", "y", "z"), grad, 0, 1.0
    for phase in range(2):
        axis = order[phase]
        n, p, buffer = SIZES[axis], me[axis], slots[phase]
        near /= n
        target = along(me, axis, sign)
        for t in range(n - 1):
            source = local.at[cut(axes, axis, (p - sign + n) % n, wide)] if t == 0 else buffer.at[t - 1]
            copy = pltpu.make_async_remote_copy(
                src_ref=source,
                dst_ref=buffer.at[t],
                send_sem=sends.at[copy_number],
                recv_sem=recvs.at[copy_number],
                device_id=target,
                device_id_type=MESH,
            )
            copy.start()
            drain.append(copy)
            copy_number += 1
            yield 2.2 + 45.0 * near
            copy.wait_recv()
            add_into(buffer.at[t], local, cut(axes, axis, (p - sign * (t + 2) + 2 * n) % n, wide))
        local = buffer.at[n - 2]
        axes = tuple(a for a in axes if a != axis)
    axis = order[2]
    n, p, buffer = SIZES[axis], me[axis], slots[2]
    copies = []
    for delta in range(1, n):
        copy = pltpu.make_async_remote_copy(
            src_ref=local.at[cut(axes, axis, (p + delta) % n, wide)],
            dst_ref=buffer.at[delta - 1],
            send_sem=sends.at[copy_number],
            recv_sem=recvs.at[copy_number],
            device_id=along(me, axis, delta),
            device_id_type=MESH,
        )
        copy.start()
        drain.append(copy)
        copies.append(copy)
        copy_number += 1
    yield 1.0 + 0.9 * n
    total = local[cut(axes, axis, p, wide)].astype(jnp.float32)
    for delta in range(1, n):
        copies[delta - 1].wait_recv()
        total = total + buffer[delta - 1].astype(jnp.float32)
    out[...] = total.astype(out.dtype)


def scatter_kernel(*refs):
    grads, outs, rest = refs[:6], refs[6:9], refs[9:]
    me = position()
    meet(me)
    drain, waiting = [], []
    for number in range(6):
        which, layer_number = number % 3, number // 3
        slots, sends, recvs = rest[5 * number : 5 * number + 3], rest[5 * number + 3], rest[5 * number + 4]
        one = reduce_one(
            me, number, which < 2, ORDERS[which], 1 - 2 * layer_number, grads[number], slots, sends, recvs, outs[which].at[layer_number], drain
        )
        waiting.append((next(one), number, one))
    heapq.heapify(waiting)
    while waiting:
        now, number, one = heapq.heappop(waiting)
        step = next(one, None)
        if step is not None:
            heapq.heappush(waiting, (now + step, number, one))
    for copy in drain:
        copy.wait_send()


def reduce_scatter(grads):
    scratch = []
    for number in range(6):
        which = number % 3
        axes, count = ("x", "y", "z"), 0
        for phase in range(3):
            n = SIZES[ORDERS[which][phase]]
            axes = tuple(a for a in axes if a != ORDERS[which][phase])
            scratch.append(pltpu.VMEM((n - 1,) + shape_of(axes, which < 2), jnp.bfloat16))
            count += n - 1
        scratch += [pltpu.SemaphoreType.DMA((count,))] * 2
    return pl.pallas_call(
        scatter_kernel,
        out_shape=[jax.ShapeDtypeStruct((2, 16, LANES), jnp.bfloat16)] * 3,
        in_specs=[pl.BlockSpec(memory_space=pltpu.VMEM)] * 6,
        out_specs=[pl.BlockSpec(memory_space=pltpu.VMEM)] * 3,
        scratch_shapes=scratch,
        compiler_params=pltpu.CompilerParams(collective_id=0, has_side_effects=True, vmem_limit_bytes=40 << 20),
        name="reduce_scatter",
    )(*grads)


def norm_kernel(count, a_ref, b_ref, c_ref, factor_ref, *rest):
    slots, sends, recvs = rest[:3], rest[3], rest[4]
    me = position()
    meet(me)
    total = jnp.zeros((8, 128), jnp.float32)
    for ref in (a_ref, b_ref, c_ref):
        for number in range(2):
            wide = ref[number].astype(jnp.float32)
            wide = wide * wide
            for rows in range(0, 16, 8):
                for columns in range(0, LANES, 128):
                    total = total + wide[rows : rows + 8, columns : columns + 128]
    copy_number, drain = 0, []
    for (axis, n), buffer in zip(SIZES.items(), slots, strict=True):
        p = me[axis]
        buffer[p] = total
        copies = []
        for delta in range(1, n):
            copy = pltpu.make_async_remote_copy(
                src_ref=buffer.at[p],
                dst_ref=buffer.at[p],
                send_sem=sends.at[copy_number],
                recv_sem=recvs.at[copy_number],
                device_id=along(me, axis, delta),
                device_id_type=MESH,
            )
            copy.start()
            copies.append(copy)
            copy_number += 1
        for copy in copies:
            copy.wait_recv()
        total = buffer[0]
        for i in range(1, n):
            total = total + buffer[i]
        drain += copies
    mean = jnp.sum(total, keepdims=True) / count
    factor_ref[...] = jnp.broadcast_to(jnp.minimum(1.0, 0.5 * lax.rsqrt(mean + 1e-30)), factor_ref.shape)
    for copy in drain:
        copy.wait_send()


def clip_factor(shares, count):
    copies = sum(n - 1 for n in SIZES.values())
    return pl.pallas_call(
        functools.partial(norm_kernel, count),
        out_shape=jax.ShapeDtypeStruct((8, 128), jnp.float32),
        in_specs=[pl.BlockSpec(memory_space=pltpu.VMEM)] * 3,
        out_specs=pl.BlockSpec(memory_space=pltpu.VMEM),
        scratch_shapes=[pltpu.VMEM((n, 8, 128), jnp.float32) for n in SIZES.values()] + [pltpu.SemaphoreType.DMA((copies,))] * 2,
        compiler_params=pltpu.CompilerParams(collective_id=1, has_side_effects=True, vmem_limit_bytes=4 << 20),
        cost_estimate=pl.CostEstimate(flops=20_000_000, bytes_accessed=200_000, transcendentals=0),
        name="clip_factor",
    )(*shares)


def adamw_kernel(wide, factor_ref, g_ref, w_ref, m_ref, v_ref, w_out, m_out, v_out):
    factor = factor_ref[0:1, 0:1]
    rows = w_ref.shape[1]
    across = 4 if wide else 1

    def body(r, _):
        here = pl.ds(pl.multiple_of(r * 16, 16), 16)
        for k in range(across):
            columns = pl.ds(k * LANES, LANES)
            g = g_ref[0, r * across + k].astype(jnp.float32) * factor
            m = 0.9 * m_ref[0, here, columns] + 0.1 * g
            v = 0.95 * v_ref[0, here, columns] + 0.05 * g * g
            w = w_ref[0, here, columns].astype(jnp.float32)
            step = m * lax.rsqrt(v + 1e-8) + 0.1 * w
            w_out[0, here, columns] = (w - 0.02 * step).astype(jnp.bfloat16)
            m_out[0, here, columns] = m
            v_out[0, here, columns] = v
        return 0

    lax.fori_loop(0, rows // 16, body, 0, unroll=2)


def adamw(w, m, v, g, factor):
    layers, rows, columns = w.shape
    wide = columns > LANES
    block = min(rows, 262144 // columns)
    tiles = block // 16 * (columns // LANES)
    whole = pl.BlockSpec((1, block, columns), lambda i, j: (i, j, 0))
    size = w.size
    return pl.pallas_call(
        functools.partial(adamw_kernel, wide),
        grid=(layers, rows // block),
        out_shape=[jax.ShapeDtypeStruct(w.shape, t) for t in (jnp.bfloat16, jnp.float32, jnp.float32)],
        in_specs=[pl.BlockSpec((8, 128), lambda i, j: (0, 0)), pl.BlockSpec((1, tiles, 16, LANES), lambda i, j: (i, j, 0, 0)), whole, whole, whole],
        out_specs=[whole] * 3,
        compiler_params=pltpu.CompilerParams(vmem_limit_bytes=63 << 20),
        cost_estimate=pl.CostEstimate(flops=16 * size, bytes_accessed=22 * size, transcendentals=size),
        name="adamw",
    )(factor, g, w, m, v)


def optimizer(grads, weights, m, v):
    count = sum(w.size for w in weights)
    x, y, z = SIZES.values()
    cutup = [g.reshape((x, y, z, 16, LANES) if i % 3 == 2 else (x, y, z // 4, 16, 4 * LANES)) for i, g in enumerate(grads)]
    shares = reduce_scatter(cutup)
    gathered = [lax.all_gather(s, "dp", axis=1, tiled=True).reshape(2, -1, 16, LANES) for s in shares]
    factor = clip_factor(shares, count)
    new = [adamw(w, m, v, g, factor) for w, m, v, g in zip(weights, m, v, gathered, strict=True)]
    return tuple(one[which] for which in range(3) for one in new)


def solution(mesh):
    def step(x, dy, *arrays):
        weights, m, v = (arrays[i : i + 3] for i in (0, 3, 6))
        layers = weights[0].shape[0]
        h, kept = x[0], []
        for number in range(layers):
            kept.append(h)
            h = layer(h, {name: w[number] for name, w in zip(NAMES, weights, strict=True)})
        by_h, grads = dy[0], [None] * layers
        for number in reversed(range(layers)):
            _, back = jax.vjp(lambda w, h: layer(h, w), {name: w[number] for name, w in zip(NAMES, weights, strict=True)}, kept[number])
            by_w, by_h = back(by_h)
            grads[number] = [by_w[name] for name in NAMES]
        return optimizer(grads[0] + grads[1], weights, m, v)

    return jax.shard_map(
        step,
        mesh=mesh,
        in_specs=(P(("rep", "dp"), None, None),) * 2 + (P(None, None, None),) * 9,
        out_specs=(P("rep", None, None),) * 9,
        check_vma=False,
    )
```

time: 585 us -> 672 us (1.15)
  Pallas kernels: 0 us -> 158 us
  other arithmetic: 56.6 us -> 1.89 us
  waiting for transfers between devices: 318 us -> 294 us
  local copies, waits for them, and re-layouts: 8.48 us -> 15.5 us
    psum x1 -> x0, waiting for transfers between devices: 318 us -> none  [step(): summed[number] = [lax.psum(by_w[name], 'dp') for name in NAMES]]
    all_gather x0 -> x3, waiting for transfers between devices: none -> 293 us  [optimizer(): lax.all_gather(s, 'dp', axis=1, tiled=True).reshape(2, -1, 16, LANES)]
    pallas_call x0 -> x5, Pallas kernels: none -> 158 us  [the longest x1 83.9 us: reduce_scatter(): pl.pallas_call(scatter_kernel, out_shape=[jax.ShapeDtypeStruct((2, 16, LA...]
    convert_element_type x2 -> x0, other arithmetic: 43.2 us -> none  [adamw(): return ((w - 0.02 * step).astype(jnp.bfloat16), m, v)]
    reduce_sum x3 -> x0, other arithmetic: 11.5 us -> none  [step(): jnp.sum(g * g)]
    dot_general x5, matrix products: 48.6 us -> 41.4 us  [matmul(): jnp.dot(a, w, preferred_element_type=jnp.float32).astype(jnp.bfloat16)]
    dot_general x5, matrix products: 67.3 us -> 74.4 us  [layer(): gate = jnp.dot(a, w['w_gate'], preferred_element_type=jnp.float32)]
    unnamed x46 -> x56, local copies, waits for them, and re-layouts: 8.48 us -> 15.5 us
  transfers between devices with their start and end apart: 1 -> 3, of which waited for: 1 -> 3; matrix products, arithmetic and copies ran while one was open for 0% -> 0% of each run, Pallas kernels for 0% -> 8%
where the time goes in v1:
time: 672 us; the launch traced here: 664 us
  waiting for transfers between devices  294 us (44%)
  matrix products  179 us (27%)
  Pallas kernels  158 us (24%)
  local copies, waits for them, and re-layouts  15.5 us (2%)
  between operations  14.5 us (2%)
    all_gather x3, waiting for transfers between devices, optimizer(): lax.all_gather(s, 'dp', axis=1, tiled=True).reshape(2, -1, 16, LANES)  293 us
    pallas_call x1, Pallas kernels, reduce_scatter(): pl.pallas_call(scatter_kernel, out_shape=[jax.ShapeDtypeStruct((2, 16, LA...  83.9 us
    dot_general x5, matrix products, layer(): gate = jnp.dot(a, w['w_gate'], preferred_element_type=jnp.float32)  74.4 us
    dot_general x5, matrix products, layer(): up = jnp.dot(a, w['w_up'], preferred_element_type=jnp.float32)  63.6 us
    pallas_call x3, Pallas kernels, adamw(): pl.pallas_call(functools.partial(adamw_kernel, wide), grid=(layers, rows...  58.5 us
    dot_general x5, matrix products, matmul(): jnp.dot(a, w, preferred_element_type=jnp.float32).astype(jnp.bfloat16)  41.4 us
    pallas_call x1, Pallas kernels, clip_factor(): pl.pallas_call(functools.partial(norm_kernel, count), out_shape=jax.Shape...  16 us
    unnamed x56, local copies, waits for them, and re-layouts  15.5 us
  transfers between devices with their start and end apart: 3, of which 3 were waited for; matrix products, arithmetic and copies ran while one was open for 0% of the time, Pallas kernels for 8%

profile of v1, /device:TPU:2, one launch (start us, length us, event | category | flops | bytes accessed | tf_op | source)
XLA Modules:
  0.0 663.8 jit_solution(6035879522400133418)
XLA Ops:
  7.2 0.0 all-gather.8.cloned.1.call-start
  7.2 2.9 copy.20
  10.2 0.0 copy-start.6
  10.2 0.5 fusion.15
  10.6 0.0 copy-start.14
  10.7 12.8 %fusion.47 = f32[2048,2048]{1,0:T(8,128)} fusion(bf16[2,512,2048]{2,1,0:T(8,128)(2,1)} %w_ref.3, bf16[1,2048,512]{2,1,0:T(8,128)(2,1)} %param.11, f32[2048]{0:T(1024)S(1)} %add_rsqrt_fusion), kind=kOutput, calls=%fused_computation.67 | convolution fusion | flops 4298113024 | bytes 20979712 | tf_op jit(solution)/shard_map/dot_general | solution.py:30
  23.5 0.0 copy-done.21
  23.5 0.0 copy-done.14
  23.5 17.2 %multiply_convert_fusion.1 = (bf16[2048,2048]{1,0:T(8,128)(2,1)}, f32[2048,2048]{1,0:T(8,128)}) fusion(f32[2048,2048]{1,0:T(8,128)} %fusion.47, bf16[2,512,2048]{2,1,0:T(8,128)(2,1)} %w_ref.4, bf16[1,2048,512]{2,1,0:T(8,128)(2,1)S(1)} %copy-done.14, f32[2048]{0:T(1024)S(1)} %add_rsqrt_fusion), kind=kOutput, calls=%fused_computation.17 | convolution fusion | flops 4323278848 | bytes 46145536 | tf_op jit(solution)/shard_map/dot_general | solution.py:31
  40.7 0.0 copy-done.6
  40.7 9.1 %fusion.19 = (f32[2048]{0:T(1024)S(1)}, bf16[2048,512]{0,1:T(8,128)(2,1)S(1)}) fusion(bf16[2048,2048]{1,0:T(8,128)(2,1)} %get-tuple-element.33, bf16[2,2048,512]{2,1,0:T(8,128)(2,1)} %w_ref.5, bf16[1,2048,512]{1,2,0:T(8,128)(2,1)S(1)} %copy.20), kind=kOutput, calls=%fused_computation.37 | convolution fusion | flops 4300208128 | bytes 14688256 | tf_op jit(solution)/shard_map/dot_general | solution.py:19
  49.8 0.0 copy-start.19
  49.8 0.0 copy-start.16
  49.9 0.0 copy-done.9
  49.9 0.0 copy-done.15
  49.9 0.0 copy-start.11
  49.9 7.4 %convolution_convert_fusion.1 = bf16[2048,2048]{1,0:T(8,128)(2,1)} fusion(bf16[1,2048,512]{2,1,0:T(8,128)(2,1)S(1)} %copy-done.15, bf16[2,2048,512]{2,1,0:T(8,128)(2,1)S(1)} %copy-done.9), kind=kOutput, calls=%fused_computation.25 | convolution fusion | flops 4299161600 | bytes 12582912 | tf_op jit(solution)/shard_map/transpose(jvp())/dot_general | solution.py:19
  57.3 0.0 copy-done.19
  57.3 0.0 copy-done.16
  57.3 0.0 copy-done.11
  57.3 8.1 %fusion.36 = f32[2048,2048]{1,0:T(8,128)} fusion(bf16[2,512,2048]{2,1,0:T(8,128)(2,1)S(1)} %copy-done.11, bf16[2048,512]{0,1:T(8,128)(2,1)S(1)} %get-tuple-element.36, f32[2048]{0:T(1024)S(1)} %fusion.66), kind=kOutput, calls=%fused_computation.56 | convolution fusion | flops 4298113024 | bytes 20979712 | tf_op jit(solution)/shard_map/jvp()/dot_general | solution.py:31
  65.4 22.7 %fusion.2 = (bf16[2048,2048]{1,0:T(8,128)(2,1)}, f32[2048,2048]{1,0:T(8,128)}) fusion(f32[2048,2048]{1,0:T(8,128)} %fusion.36, bf16[2048,2048]{1,0:T(8,128)(2,1)} %convolution_convert_fusion.1, bf16[2,512,2048]{2,1,0:T(8,128)(2,1)} %w_ref.3, bf16[2048,512]{0,1:T(8,128)(2,1)} %copy-done.16, f32[2048]{0:T(1024)S(1)} %fusion.66), kind=kOutput, calls=%fused_computation.8 | convolution fusion | flops 4348444672 | bytes 54534144 | tf_op jit(solution)/shard_map/jvp()/dot_general | solution.py:30
  88.1 13.7 %fusion.22 = bf16[2048,512]{1,0:T(8,128)(2,1)S(1)} fusion(f32[2048,2048]{1,0:T(8,128)} %fusion.36, bf16[1,2048,512]{2,1,0:T(8,128)(2,1)} %param.12, f32[2048,2048]{1,0:T(8,128)} %get-tuple-element.38), kind=kOutput, calls=%fused_computation.41 | convolution fusion | flops 4321181696 | bytes 37748736 | tf_op jit(solution)/shard_map/transpose(jvp())/dot_general | solution.py:19
  101.8 0.0 copy-done.17
  101.8 0.0 copy-start.12
  101.9 12.5 %fusion.27 = bf16[512,2048]{1,0:T(8,128)(2,1)} fusion(bf16[2048,2048]{1,0:T(8,128)(2,1)} %convolution_convert_fusion.1, bf16[2048,512]{0,1:T(8,128)(2,1)S(1)} %copy-done.17, f32[2048]{0:T(1024)S(1)} %fusion.66, f32[2048,2048]{1,0:T(8,128)} %get-tuple-element.38), kind=kOutput, calls=%fused_computation.46 | convolution fusion | flops 4324327424 | bytes 29368320 | tf_op jit(solution)/shard_map/transpose(jvp())/dot_general | solution.py:31
  114.4 0.0 copy-done.12
  114.4 12.1 %fusion.26 = bf16[2048,512]{0,1:T(8,128)(2,1)} fusion(bf16[2048,2048]{1,0:T(8,128)(2,1)} %convolution_convert_fusion.1, bf16[2,512,2048]{2,1,0:T(8,128)(2,1)S(1)} %copy-done.12, f32[2048,2048]{1,0:T(8,128)} %get-tuple-element.38), kind=kOutput, calls=%fused_computation.45 | convolution fusion | flops 4321181696 | bytes 29360128 | tf_op jit(solution)/shard_map/transpose(jvp())/dot_general | solution.py:31
  126.5 3.9 copy.21
  130.5 10.0 %convolution_convert_fusion.4 = bf16[512,2048]{1,0:T(8,128)(2,1)} fusion(bf16[2048,2048]{1,0:T(8,128)(2,1)} %get-tuple-element.37, bf16[2048,512]{0,1:T(8,128)(2,1)} %copy-done.16, f32[2048]{0:T(1024)S(1)} %fusion.66), kind=kOutput, calls=%fused_computation.48 | convolution fusion | flops 4298113024 | bytes 12591104 | tf_op jit(solution)/shard_map/transpose(jvp())/dot_general | solution.py:30
  140.4 0.0 copy-done.13
  140.4 0.0 copy-done.18
  140.4 0.0 copy-done.24
  140.5 0.0 copy-start.20
  140.5 0.0 copy-start.8
  140.5 0.0 slice-start.1
  140.5 9.2 %fusion.21 = (f32[2048]{0:T(1024)S(1)}, bf16[2048,512]{0,1:T(8,128)(2,1)S(1)}) fusion(bf16[2048,512]{0,1:T(8,128)(2,1)S(1)} %copy-done.18, bf16[2048,512]{0,1:T(8,128)(2,1)S(1)} %copy-done.24, bf16[2048,2048]{1,0:T(8,128)(2,1)} %get-tuple-element.37, bf16[2,512,2048]{2,1,0:T(8,128)(2,1)S(1)} %copy-done.13), kind=kOutput, calls=%fused_computation.39 | convolution fusion | flops 4300208128 | bytes 16785408 | tf_op jit(solution)/shard_map/transpose(jvp())/dot_general | solution.py:30
  149.8 1.4 fusion.33
  151.2 0.0 copy-start.10
  151.2 6.4 convolution_convert_fusion.2
  157.6 0.0 copy-done.10
  157.6 4.9 convolution_convert_fusion
  162.5 0.0 copy-start.23
  162.5 13.5 %fusion.28 = bf16[512,2048]{1,0:T(8,128)(2,1)} fusion(bf16[2048,2048]{1,0:T(8,128)(2,1)S(1)} %convolution_convert_fusion, f32[2048,2048]{1,0:T(8,128)} %fusion.47, bf16[1,2048,512]{1,2,0:T(8,128)(2,1)S(1)} %copy-done.7, f32[2048]{0:T(1024)S(1)} %copy-done.22), kind=kOutput, calls=%fused_computation.47 | convolution fusion | flops 4324327424 | bytes 29368320 | tf_op jit(solution)/shard_map/transpose(jvp())/dot_general | solution.py:31
  176.0 19.7 %fusion.23 = bf16[512,2048]{1,0:T(8,128)(2,1)} fusion(f32[2048,2048]{1,0:T(8,128)} %fusion.47, f32[2048,2048]{1,0:T(8,128)} %get-tuple-element.34, bf16[2048,2048]{1,0:T(8,128)(2,1)} %copy-done.23, bf16[1,2048,512]{1,2,0:T(8,128)(2,1)} %copy-done.6, f32[2048]{0:T(1024)S(1)} %copy-done.22), kind=kOutput, calls=%fused_computation.42 | convolution fusion | flops 4345298944 | bytes 46145536 | tf_op jit(solution)/shard_map/transpose(jvp())/dot_general | solution.py:30
  195.8 1.6 copy-done
  197.4 1.6 copy-done.1
  199.0 1.6 copy-done.2
  200.6 1.6 copy-done.3
  202.1 1.6 copy-done.4
  203.7 83.9 %reduce_scatter.1 = (bf16[2,16,512]{2,1,0:T(8,128)(2,1)}, bf16[2,16,512]{2,1,0:T(8,128)(2,1)}, bf16[2,16,512]{2,1,0:T(8,128)(2,1)}) custom-call(bf16[4,4,2,16,2048]{4,3,2,1,0:T(8,128)(2,1)S(1)} %bitcast.72, bf16[4,4,2,16,2048]{4,3,2,1,0:T(8,128)(2,1)S(1)} %bitcast.71, bf16[4,4,8,16,512]{4,3,2,1,0:T(8,128)(2,1)S(1)} %bitcast.70, ...), custom_call_target="tpu_custom_call" | custom-call | tf_op jit(solution)/shard_map/reduce_scatter/pallas_call | solution.py:177
  287.6 0.0 all-gather.8.cloned.1.call-update
  287.6 0.0 all-gather.6.cloned.1.call-start
  287.7 0.7 all-gather.6.cloned.1.call-update
  288.4 0.0 all-gather.4.cloned.1.call-start
  288.4 0.7 all-gather.4.cloned.1.call-update
  289.1 16.0 %clip_factor.1.factor_ref = f32[8,128]{1,0:T(8,128)S(1)} custom-call(bf16[2,16,512]{2,1,0:T(8,128)(2,1)} %get-tuple-element.21.a_ref, bf16[2,16,512]{2,1,0:T(8,128)(2,1)} %get-tuple-element.22.b_ref, bf16[2,16,512]{2,1,0:T(8,128)(2,1)} %get-tuple-element.23.c_ref), custom_call_target="tpu_custom_call" | custom-call | flops 20000000 | bytes 200000 | tf_op jit(solution)/shard_map/clip_factor/pallas_call | solution.py:231
  305.1 0.6 copy-done.5
  305.7 97.2 %all-gather.8.cloned.1.call-done = bf16[2,2048,512]{2,1,0:T(8,128)(2,1)} async-done(((bf16[2,16,512]{2,1,0:T(8,128)(2,1)}), bf16[2,2048,512]{2,1,0:T(8,128)(2,1)}) %all-gather.8.cloned.1.call-update) | async-done | bytes 4194320 | tf_op jit(solution)/shard_map/all_gather | solution.py:289
  402.9 20.9 %adamw.5 = (bf16[2,2048,512]{2,1,0:T(8,128)(2,1)}, f32[2,2048,512]{2,1,0:T(8,128)}, f32[2,2048,512]{2,1,0:T(8,128)}) custom-call(f32[8,128]{1,0:T(8,128)} %copy-done.5, bf16[2,128,16,512]{3,2,1,0:T(8,128)(2,1)} %bitcast.73, bf16[2,2048,512]{2,1,0:T(8,128)(2,1)} %w_ref.5, f32[2,2048,512]{2,1,0:T(8,128)} %m_ref.5, f32[2,2048,512]{2,1,0:T(8,128)} %v_ref.5), custom_call_target="tpu_custom_call" | custom-call | flops 33554432 | bytes 46137344 | tf_op jit(solution)/shard_map/adamw/pallas_call | solution.py:272
  423.8 96.7 %all-gather.6.cloned.1.call-done = bf16[2,2048,512]{2,1,0:T(8,128)(2,1)} async-done(((bf16[2,16,512]{2,1,0:T(8,128)(2,1)}), bf16[2,2048,512]{2,1,0:T(8,128)(2,1)}) %all-gather.6.cloned.1.call-update) | async-done | bytes 4194320 | tf_op jit(solution)/shard_map/all_gather | solution.py:289
  520.4 18.8 %adamw.4 = (bf16[2,512,2048]{2,1,0:T(8,128)(2,1)}, f32[2,512,2048]{2,1,0:T(8,128)}, f32[2,512,2048]{2,1,0:T(8,128)}) custom-call(f32[8,128]{1,0:T(8,128)} %copy-done.5, bf16[2,128,16,512]{3,2,1,0:T(8,128)(2,1)} %bitcast.74, bf16[2,512,2048]{2,1,0:T(8,128)(2,1)} %w_ref.4, f32[2,512,2048]{2,1,0:T(8,128)} %m_ref.4, f32[2,512,2048]{2,1,0:T(8,128)} %v_ref.4), custom_call_target="tpu_custom_call" | custom-call | flops 33554432 | bytes 46137344 | tf_op jit(solution)/shard_map/adamw/pallas_call | solution.py:272
  539.2 98.8 %all-gather.4.cloned.1.call-done = bf16[2,2048,512]{2,1,0:T(8,128)(2,1)} async-done(((bf16[2,16,512]{2,1,0:T(8,128)(2,1)}), bf16[2,2048,512]{2,1,0:T(8,128)(2,1)}) %all-gather.4.cloned.1.call-update) | async-done | bytes 4194320 | tf_op jit(solution)/shard_map/all_gather | solution.py:289
  638.0 18.8 %adamw.3 = (bf16[2,512,2048]{2,1,0:T(8,128)(2,1)}, f32[2,512,2048]{2,1,0:T(8,128)}, f32[2,512,2048]{2,1,0:T(8,128)}) custom-call(f32[8,128]{1,0:T(8,128)} %copy-done.5, bf16[2,128,16,512]{3,2,1,0:T(8,128)(2,1)} %bitcast.75, bf16[2,512,2048]{2,1,0:T(8,128)(2,1)} %w_ref.3, f32[2,512,2048]{2,1,0:T(8,128)} %m_ref.3, f32[2,512,2048]{2,1,0:T(8,128)} %v_ref.3), custom_call_target="tpu_custom_call" | custom-call | flops 33554432 | bytes 46137344 | tf_op jit(solution)/shard_map/adamw/pallas_call | solution.py:272
  (27 shorter events, 0.1 us)
Async XLA Ops:
  7.2 395.7 %all-gather.8.cloned.1.call-start = ((), (), s32[]{:S(2)}) async-start(), calls=%async_computation.2 | async-start | bytes 4227072 | tf_op jit(solution)/shard_map/all_gather | solution.py:289
  10.2 30.6 %copy-start.6 = (bf16[1,2048,512]{1,2,0:T(8,128)(2,1)}, bf16[1,2048,512]{1,2,0:T(8,128)(2,1)S(1)}, u32[]{:S(2)}) copy-start(bf16[1,2048,512]{1,2,0:T(8,128)(2,1)S(1)} %copy.20) | copy-start | bytes 6291460
  10.6 12.9 %copy-start.21 = (f32[2048]{0:T(1024)}, f32[2048]{0:T(1024)S(1)}, u32[]{:S(2)}) copy-start(f32[2048]{0:T(1024)S(1)} %add_rsqrt_fusion) | copy-start | bytes 24580
  10.6 12.9 %copy-start.14 = (bf16[1,2048,512]{2,1,0:T(8,128)(2,1)S(1)}, bf16[1,2048,512]{2,1,0:T(8,128)(2,1)}, u32[]{:S(2)}) copy-start(bf16[1,2048,512]{2,1,0:T(8,128)(2,1)} %param.11) | copy-start | bytes 6291460
  40.7 9.1 %copy-start.9 = (bf16[2,2048,512]{2,1,0:T(8,128)(2,1)S(1)}, bf16[2,2048,512]{2,1,0:T(8,128)(2,1)}, u32[]{:S(2)}) copy-start(bf16[2,2048,512]{2,1,0:T(8,128)(2,1)} %w_ref.5) | copy-start | bytes 12582916
  40.7 9.1 %copy-start.15 = (bf16[1,2048,512]{2,1,0:T(8,128)(2,1)S(1)}, bf16[1,2048,512]{2,1,0:T(8,128)(2,1)}, u32[]{:S(2)}) copy-start(bf16[1,2048,512]{2,1,0:T(8,128)(2,1)} %param.12) | copy-start | bytes 6291460
  49.8 7.4 %copy-start.19 = (f32[2048]{0:T(1024)}, f32[2048]{0:T(1024)S(1)}, u32[]{:S(2)}) copy-start(f32[2048]{0:T(1024)S(1)} %get-tuple-element.35) | copy-start | bytes 24580
  49.8 7.4 %copy-start.16 = (bf16[2048,512]{0,1:T(8,128)(2,1)}, bf16[2048,512]{0,1:T(8,128)(2,1)S(1)}, u32[]{:S(2)}) copy-start(bf16[2048,512]{0,1:T(8,128)(2,1)S(1)} %get-tuple-element.36) | copy-start | bytes 6291460
  49.9 7.4 %copy-start.11 = (bf16[2,512,2048]{2,1,0:T(8,128)(2,1)S(1)}, bf16[2,512,2048]{2,1,0:T(8,128)(2,1)}, u32[]{:S(2)}) copy-start(bf16[2,512,2048]{2,1,0:T(8,128)(2,1)} %w_ref.4) | copy-start | bytes 12582916
  88.1 13.7 %copy-start.17 = (bf16[2048,512]{0,1:T(8,128)(2,1)S(1)}, bf16[2048,512]{0,1:T(8,128)(2,1)}, u32[]{:S(2)}) copy-start(bf16[2048,512]{0,1:T(8,128)(2,1)} %copy-done.16) | copy-start | bytes 6291460
  101.8 12.6 %copy-start.12 = (bf16[2,512,2048]{2,1,0:T(8,128)(2,1)S(1)}, bf16[2,512,2048]{2,1,0:T(8,128)(2,1)}, u32[]{:S(2)}) copy-start(bf16[2,512,2048]{2,1,0:T(8,128)(2,1)} %w_ref.4) | copy-start | bytes 12582916
  130.5 10.0 %copy-start.13 = (bf16[2,512,2048]{2,1,0:T(8,128)(2,1)S(1)}, bf16[2,512,2048]{2,1,0:T(8,128)(2,1)}, u32[]{:S(2)}) copy-start(bf16[2,512,2048]{2,1,0:T(8,128)(2,1)} %w_ref.3) | copy-start | bytes 12582916
  130.5 10.0 %copy-start.18 = (bf16[2048,512]{0,1:T(8,128)(2,1)S(1)}, bf16[2048,512]{0,1:T(8,128)(2,1)}, u32[]{:S(2)}) copy-start(bf16[2048,512]{0,1:T(8,128)(2,1)} %copy-done.16) | copy-start | bytes 6291460
  130.5 10.0 %copy-start.24 = (bf16[2048,512]{0,1:T(8,128)(2,1)S(1)}, bf16[2048,512]{0,1:T(8,128)(2,1)}, u32[]{:S(2)}) copy-start(bf16[2048,512]{0,1:T(8,128)(2,1)} %fusion.26) | copy-start | bytes 6291460
  130.5 20.7 %slice-start = ((s8[8388608]{0:T(1024)(128)(4,1)}), s8[4194304]{0:T(1024)(128)(4,1)S(1)}, s32[]{:S(2)}) async-start(s8[8388608]{0:T(1024)(128)(4,1)} %bitcast.76), calls=%async_computation.3 | async-start | bytes 8388608
  140.5 9.3 %copy-start.20 = (f32[2048]{0:T(1024)S(1)}, f32[2048]{0:T(1024)}, u32[]{:S(2)}) copy-start(f32[2048]{0:T(1024)} %copy-done.19) | copy-start | bytes 24580
  140.5 9.3 %copy-start.8 = (bf16[1,2048,512]{1,2,0:T(8,128)(2,1)S(1)}, bf16[1,2048,512]{1,2,0:T(8,128)(2,1)}, u32[]{:S(2)}) copy-start(bf16[1,2048,512]{1,2,0:T(8,128)(2,1)} %copy.21) | copy-start | bytes 6291460
  140.5 10.7 %slice-start.1 = ((s8[8388608]{0:T(1024)(128)(4,1)}), s8[4194304]{0:T(1024)(128)(4,1)S(1)}, s32[]{:S(2)}) async-start(s8[8388608]{0:T(1024)(128)(4,1)} %bitcast.76), calls=%async_computation.4 | async-start | bytes 8388608
  151.2 6.4 copy-start.10
  157.6 4.9 copy-start.7
  157.6 4.9 copy-start.22
  162.5 13.6 %copy-start.23 = (bf16[2048,2048]{1,0:T(8,128)(2,1)}, bf16[2048,2048]{1,0:T(8,128)(2,1)S(1)}, u32[]{:S(2)}) copy-start(bf16[2048,2048]{1,0:T(8,128)(2,1)S(1)} %convolution_convert_fusion) | copy-start | bytes 25165828
  195.8 1.6 copy-start
  197.4 1.6 copy-start.1
  199.0 1.6 copy-start.2
  200.6 1.6 copy-start.3
  202.1 1.6 copy-start.4
  287.6 232.8 %all-gather.6.cloned.1.call-start = ((), (), s32[]{:S(2)}) async-start(), calls=%async_computation.1 | async-start | bytes 4227072 | tf_op jit(solution)/shard_map/all_gather | solution.py:289
  288.4 349.6 %all-gather.4.cloned.1.call-start = ((), (), s32[]{:S(2)}) async-start(), calls=%async_computation | async-start | bytes 4227072 | tf_op jit(solution)/shard_map/all_gather | solution.py:289
  305.1 0.6 copy-start.5
Sparse Core Ops, SparseCore 0:
  287.8 115.0 all-gather.7
  406.4 113.9 all-gather.5
  524.0 113.9 all-gather.3

commit v2 on v0

v2 whole, which is shorter than its diff:
```python
import functools
import heapq

import jax
import jax.numpy as jnp
from jax import lax
from jax.experimental import pallas as pl
from jax.experimental.pallas import tpu as pltpu
from jax.sharding import PartitionSpec as P

NAMES = ("w_gate", "w_up", "w_down")
SIZES = {"x": 4, "y": 4, "z": 8}
LANES = 512
MESH = pl.DeviceIdType.MESH
ORDERS = (("x", "y", "z"), ("y", "z", "x"), ("z", "x", "y"))


TOKENS = 512
HIDDEN = 256


def dot(a, b, on=(1, 0)):
    return lax.dot_general(a, b, (((on[0],), (on[1],)), ((), ())), preferred_element_type=jnp.float32)


def gradients_kernel(x_ref, dy_ref, wg_ref, wu_ref, wd_ref, *refs):
    (gg0, gu0, gd0, gg1, gu1, gd1), (a_ref, h_ref, b_ref, hid_ref, dgate_ref, dup_ref, one_ref, two_ref) = refs[:6], refs[6:]
    tokens, d = x_ref.shape
    ff = wg_ref.shape[2]

    def over(n, size, body):
        def at_step(i, _):
            body(pl.ds(pl.multiple_of(i * size, size), size))
            return 0

        lax.fori_loop(0, n // size, at_step, 0)

    def norm(source, target):
        def rows(t):
            wide = source[t, :].astype(jnp.float32)
            target[t, :] = (wide * lax.rsqrt(jnp.mean(wide * wide, -1, keepdims=True) + 1e-6)).astype(jnp.bfloat16)

        over(tokens, 128, rows)

    def zero(ref):
        def rows(t):
            ref[t, :] = jnp.zeros((128, d), jnp.float32)

        over(tokens, 128, rows)

    norm(x_ref, a_ref)
    zero(one_ref)

    def forward(f):
        def rows(t):
            a = a_ref[t, :]
            gate, up = dot(a, wg_ref[0, :, f]), dot(a, wu_ref[0, :, f])
            hidden = (gate * jax.nn.sigmoid(gate) * up).astype(jnp.bfloat16)
            one_ref[t, :] += dot(hidden, wd_ref[0, f, :])

        over(tokens, TOKENS, rows)

    over(ff, HIDDEN, forward)

    def add(t):
        h = x_ref[t, :].astype(jnp.float32) + one_ref[t, :].astype(jnp.bfloat16).astype(jnp.float32)
        h_ref[t, :] = h.astype(jnp.bfloat16)

    over(tokens, 128, add)

    def backward(number, a_ref, by_ref, gg, gu, gd, more):
        def hidden_block(f):
            def rows(t):
                a, by = a_ref[t, :], by_ref[t, :]
                gate, up = dot(a, wg_ref[number, :, f]), dot(a, wu_ref[number, :, f])
                by_hidden = dot(by, wd_ref[number, f, :], (1, 1)).astype(jnp.bfloat16).astype(jnp.float32)
                sigmoid = jax.nn.sigmoid(gate)
                silu = gate * sigmoid
                hid_ref[t, :] = (silu * up).astype(jnp.bfloat16)
                dup = (by_hidden * silu).astype(jnp.bfloat16)
                dgate = (by_hidden * up * (sigmoid + silu * (1.0 - sigmoid))).astype(jnp.bfloat16)
                dgate_ref[t, :] = dgate
                dup_ref[t, :] = dup
                if more:
                    one_ref[t, :] += dot(dgate, wg_ref[number, :, f], (1, 1))
                    two_ref[t, :] += dot(dup, wu_ref[number, :, f], (1, 1))

            over(tokens, TOKENS, rows)
            gd[f, :] = dot(hid_ref[...], by_ref[...], (0, 0)).astype(jnp.bfloat16)
            gg[:, f] = dot(a_ref[...], dgate_ref[...], (0, 0)).astype(jnp.bfloat16)
            gu[:, f] = dot(a_ref[...], dup_ref[...], (0, 0)).astype(jnp.bfloat16)

        over(ff, HIDDEN, hidden_block)

    norm(h_ref, b_ref)
    zero(one_ref)
    zero(two_ref)
    backward(1, b_ref, dy_ref, gg1, gu1, gd1, True)

    def by_norm(t):
        wide = h_ref[t, :].astype(jnp.float32)
        by = (one_ref[t, :].astype(jnp.bfloat16).astype(jnp.float32) + two_ref[t, :].astype(jnp.bfloat16).astype(jnp.float32))
        by = by.astype(jnp.bfloat16).astype(jnp.float32)
        scale = lax.rsqrt(jnp.mean(wide * wide, -1, keepdims=True) + 1e-6)
        inner = jnp.mean(by * wide, -1, keepdims=True)
        by_h = (by * scale - wide * (inner * scale * scale * scale)).astype(jnp.bfloat16).astype(jnp.float32)
        b_ref[t, :] = (dy_ref[t, :].astype(jnp.float32) + by_h).astype(jnp.bfloat16)

    over(tokens, 128, by_norm)
    backward(0, a_ref, b_ref, gg0, gu0, gd0, False)


def gradients(x, dy, w_gate, w_up, w_down):
    tokens, d = x.shape
    ff = w_gate.shape[2]
    shapes = [(d, ff), (d, ff), (ff, d)] * 2
    flops = 17 * 2 * tokens * d * ff
    return pl.pallas_call(
        gradients_kernel,
        out_shape=[jax.ShapeDtypeStruct(s, jnp.bfloat16) for s in shapes],
        in_specs=[pl.BlockSpec(memory_space=pltpu.VMEM)] * 5,
        out_specs=[pl.BlockSpec(memory_space=pltpu.VMEM)] * 6,
        scratch_shapes=[pltpu.VMEM((tokens, d), jnp.bfloat16)] * 3
        + [pltpu.VMEM((tokens, HIDDEN), jnp.bfloat16)] * 3
        + [pltpu.VMEM((tokens, d), jnp.float32)] * 2,
        compiler_params=pltpu.CompilerParams(vmem_limit_bytes=63 << 20),
        cost_estimate=pl.CostEstimate(flops=flops, bytes_accessed=30 << 20, transcendentals=3 * tokens * ff),
        name="gradients",
    )(x, dy, w_gate, w_up, w_down)


def position():
    dp = lax.axis_index("dp")
    ny, nz = SIZES["y"], SIZES["z"]
    return {"x": dp // (ny * nz), "y": (dp // nz) % ny, "z": dp % nz}


def along(me, axis, delta):
    at = dict(me)
    at[axis] = (me[axis] + delta + SIZES[axis]) % SIZES[axis]
    return {"dp": (at["x"] * SIZES["y"] + at["y"]) * SIZES["z"] + at["z"]}


def meet(me):
    barrier = pltpu.get_barrier_semaphore()
    count = 0
    for axis, n in SIZES.items():
        for delta in range(1, n):
            pl.semaphore_signal(barrier, inc=1, device_id=along(me, axis, delta), device_id_type=MESH)
            count += 1
    pl.semaphore_wait(barrier, count)


def cut(axes, axis, i, wide):
    lead = (slice(None),) * axes.index(axis)
    if wide and axis == "z":
        return lead + (i // 4, slice(None), pl.ds(pl.multiple_of((i % 4) * LANES, LANES), LANES))
    return lead + (i,)


def shape_of(axes, wide):
    if wide and "z" in axes:
        return tuple(SIZES[a] for a in axes if a != "z") + (SIZES["z"] // 4, 16, 4 * LANES)
    return tuple(SIZES[a] for a in axes) + (16, LANES)


def at(index, lead):
    out, rest = [], list(lead)
    for part in index:
        out.append(rest.pop(0) if isinstance(part, slice) and rest else part)
    return tuple(out[: len(index)]) + tuple(rest)


def add_into(slot, local, index):
    shape = slot.shape[:-2]
    total = 1
    for n in shape:
        total *= n

    def body(i, _):
        lead, rest = [], i
        for n in reversed(shape):
            lead.insert(0, rest % n)
            rest = rest // n
        term = local[at(index, lead)].astype(jnp.float32)
        slot[tuple(lead)] = (slot[tuple(lead)].astype(jnp.float32) + term).astype(slot.dtype)
        return 0

    lax.fori_loop(0, total, body, 0, unroll=False)


def region(fixed, wide):
    lead = tuple(fixed.get(axis, slice(None)) for axis in "xy")
    if "z" not in fixed:
        return lead
    if wide:
        return lead + (fixed["z"] // 4, slice(None), pl.ds(pl.multiple_of((fixed["z"] % 4) * LANES, LANES), LANES))
    return lead + (fixed["z"],)


def sum_one(me, wide, order, sign, grad, slots, sends, recvs, out, squares, drain):
    axes, local, near = ("x", "y", "z"), grad, 1.0
    numbers = iter(range(1000))

    def send(source, target, to):
        number = next(numbers)
        copy = pltpu.make_async_remote_copy(
            src_ref=source, dst_ref=target, send_sem=sends.at[number], recv_sem=recvs.at[number], device_id=to, device_id_type=MESH
        )
        copy.start()
        drain.append(copy)
        return copy

    for phase in range(2):
        axis = order[phase]
        n, p, buffer = SIZES[axis], me[axis], slots[phase]
        near /= n
        target = along(me, axis, sign)
        for t in range(n - 1):
            source = local.at[cut(axes, axis, (p - sign + n) % n, wide)] if t == 0 else buffer.at[t - 1]
            copy = send(source, buffer.at[t], target)
            yield 2.2 + 46.0 * near
            copy.wait_recv()
            add_into(buffer.at[t], local, cut(axes, axis, (p - sign * (t + 2) + 2 * n) % n, wide))
        local = buffer.at[n - 2]
        axes = tuple(a for a in axes if a != axis)
    axis = order[2]
    n, p, buffer = SIZES[axis], me[axis], slots[2]
    copies = [
        send(local.at[cut(axes, axis, (p + delta) % n, wide)], buffer.at[delta - 1], along(me, axis, delta)) for delta in range(1, n)
    ]
    yield 1.0 + 0.9 * n
    total = local[cut(axes, axis, p, wide)].astype(jnp.float32)
    for delta in range(1, n):
        copies[delta - 1].wait_recv()
        total = total + buffer[delta - 1].astype(jnp.float32)
    total = total.astype(out.dtype)
    mine = region(me, wide)
    out[mine] = total
    wide_total = total.astype(jnp.float32)
    wide_total = wide_total * wide_total
    square = jnp.zeros((8, 128), jnp.float32)
    for rows in range(0, 16, 8):
        for columns in range(0, LANES, 128):
            square = square + wide_total[rows : rows + 8, columns : columns + 128]
    squares[...] = square
    copies = [send(out.at[mine], out.at[mine], along(me, axis, delta)) for delta in range(1, n)]
    yield "reduced"
    yield 1.0 + 0.9 * n
    for copy in copies:
        copy.wait_recv()
    fixed = dict(me)
    for phase in (1, 0):
        fixed.pop(order[phase + 1])
        axis = order[phase]
        n, p = SIZES[axis], me[axis]
        target = along(me, axis, sign)
        for t in range(n - 1):
            block = out.at[region({**fixed, axis: (p - sign * t + n) % n}, wide)]
            copy = send(block, block, target)
            yield 2.2 + 46.0 * near
            copy.wait_recv()
        near *= n


def norm_one(me, count, squares, factor, slots, sends, recvs, drain):
    total = squares[0]
    for number in range(1, 6):
        total = total + squares[number]
    copy_number = 0
    for (axis, n), buffer in zip(SIZES.items(), slots, strict=True):
        p = me[axis]
        buffer[p] = total
        copies = []
        for delta in range(1, n):
            copy = pltpu.make_async_remote_copy(
                src_ref=buffer.at[p],
                dst_ref=buffer.at[p],
                send_sem=sends.at[copy_number],
                recv_sem=recvs.at[copy_number],
                device_id=along(me, axis, delta),
                device_id_type=MESH,
            )
            copy.start()
            copies.append(copy)
            copy_number += 1
        yield 1.0 + 0.9 * n
        for copy in copies:
            copy.wait_recv()
        total = buffer[0]
        for i in range(1, n):
            total = total + buffer[i]
        drain += copies
    mean = jnp.sum(total, keepdims=True) / count
    factor[...] = jnp.broadcast_to(jnp.minimum(1.0, 0.5 * lax.rsqrt(mean + 1e-30)), factor.shape)


def sum_kernel(count, *refs):
    grads, outs, factor, squares, norm, rest = refs[:6], refs[6:9], refs[9], refs[10], refs[11:16], refs[16:]
    me = position()
    meet(me)
    drain, waiting, reduced = [], [], 0
    for number in range(6):
        which, layer_number = number % 3, number // 3
        slots, sends, recvs = rest[5 * number : 5 * number + 3], rest[5 * number + 3], rest[5 * number + 4]
        sign = 1 - 2 * layer_number
        out = outs[which].at[layer_number]
        one = sum_one(me, which < 2, ORDERS[which], sign, grads[number], slots, sends, recvs, out, squares.at[number], drain)
        waiting.append((next(one), number, one))
    heapq.heapify(waiting)
    while waiting:
        now, number, one = heapq.heappop(waiting)
        step = next(one, None)
        if step == "reduced":
            reduced += 1
            if reduced == 6:
                last = norm_one(me, count, squares, factor, norm[:3], norm[3], norm[4], drain)
                heapq.heappush(waiting, (now + next(last), 6, last))
            step = next(one)
        if step is not None:
            heapq.heappush(waiting, (now + step, number, one))
    for copy in drain:
        copy.wait_send()


def sums(grads, count):
    scratch = [pltpu.VMEM((6, 8, 128), jnp.float32)] + [pltpu.VMEM((n, 8, 128), jnp.float32) for n in SIZES.values()]
    steps = sum(n - 1 for n in SIZES.values())
    scratch += [pltpu.SemaphoreType.DMA((steps,))] * 2
    for number in range(6):
        which = number % 3
        axes = ("x", "y", "z")
        for phase in range(3):
            axes = tuple(a for a in axes if a != ORDERS[which][phase])
            scratch.append(pltpu.VMEM((SIZES[ORDERS[which][phase]] - 1,) + shape_of(axes, which < 2), jnp.bfloat16))
        scratch += [pltpu.SemaphoreType.DMA((2 * steps,))] * 2
    return pl.pallas_call(
        functools.partial(sum_kernel, count),
        out_shape=[jax.ShapeDtypeStruct((2,) + shape_of(("x", "y", "z"), i < 2), jnp.bfloat16) for i in range(3)]
        + [jax.ShapeDtypeStruct((8, 128), jnp.float32)],
        in_specs=[pl.BlockSpec(memory_space=pltpu.VMEM)] * 6,
        out_specs=[pl.BlockSpec(memory_space=pltpu.VMEM)] * 4,
        scratch_shapes=scratch,
        compiler_params=pltpu.CompilerParams(collective_id=0, has_side_effects=True, vmem_limit_bytes=44 << 20),
        cost_estimate=pl.CostEstimate(flops=100_000_000_000, bytes_accessed=24 << 20, transcendentals=0),
        name="sums",
    )(*grads)


def adamw_kernel(factor_ref, *refs):
    factor = factor_ref[0:1, 0:1]
    for k in range(3):
        (g_ref, w_ref, m_ref, v_ref), (w_out, m_out, v_out) = refs[4 * k : 4 * k + 4], refs[12 + 3 * k : 15 + 3 * k]
        rows, columns = w_ref.shape[1:]

        def body(r, _):
            here = (0, pl.ds(pl.multiple_of(r * 16, 16), 16))
            for c in range(0, columns, LANES):
                at = here + (pl.ds(c, LANES),)
                g = g_ref[at].astype(jnp.float32) * factor
                m = 0.9 * m_ref[at] + 0.1 * g
                v = 0.95 * v_ref[at] + 0.05 * g * g
                w = w_ref[at].astype(jnp.float32)
                step = m * lax.rsqrt(v + 1e-8) + 0.1 * w
                w_out[at] = (w - 0.02 * step).astype(jnp.bfloat16)
                m_out[at] = m
                v_out[at] = v
            return 0

        lax.fori_loop(0, rows // 16, body, 0, unroll=max(1, LANES * 4 // columns))


def adamw(weights, m, v, g, factor, steps=8):
    blocks = [pl.BlockSpec((1, w.shape[1] // steps, w.shape[2]), lambda i, j: (i, j, 0)) for w in weights]
    size = sum(w.size for w in weights)
    shapes = [jax.ShapeDtypeStruct(w.shape, t) for w in weights for t in (jnp.bfloat16, jnp.float32, jnp.float32)]
    out = pl.pallas_call(
        adamw_kernel,
        grid=(weights[0].shape[0], steps),
        out_shape=shapes,
        in_specs=[pl.BlockSpec((8, 128), lambda i, j: (0, 0))] + [block for block in blocks for _ in range(4)],
        out_specs=[block for block in blocks for _ in range(3)],
        compiler_params=pltpu.CompilerParams(vmem_limit_bytes=63 << 20),
        cost_estimate=pl.CostEstimate(flops=16 * size, bytes_accessed=22 * size, transcendentals=size),
        name="adamw",
    )(factor, *(one for four in zip(g, weights, m, v, strict=True) for one in four))
    return [out[3 * k : 3 * k + 3] for k in range(3)]


def optimizer(grads, weights, m, v):
    count = sum(w.size for w in weights)
    cutup = [g.reshape(shape_of(("x", "y", "z"), i % 3 < 2)) for i, g in enumerate(grads)]
    *summed, factor = sums(cutup, count)
    new = adamw(weights, m, v, [s.reshape(w.shape) for s, w in zip(summed, weights, strict=True)], factor)
    return tuple(one[which] for which in range(3) for one in new)


def solution(mesh):
    def step(x, dy, *arrays):
        weights, m, v = (arrays[i : i + 3] for i in (0, 3, 6))
        return optimizer(gradients(x[0], dy[0], *weights), weights, m, v)

    return jax.shard_map(
        step,
        mesh=mesh,
        in_specs=(P(("rep", "dp"), None, None),) * 2 + (P(None, None, None),) * 9,
        out_specs=(P("rep", None, None),) * 9,
        check_vma=False,
    )
```

time: 585 us -> 342 us (0.58); the launches traced: 578 us -> 342 us
  Pallas kernels: 0 us -> 334 us
  waiting for transfers between devices: 318 us -> 0 us
  matrix products: 179 us -> 0 us
  other arithmetic: 56.6 us -> 0 us
  between operations: 16.7 us -> 0.66 us
    pallas_call x0 -> x3, Pallas kernels: none -> 334 us  [the longest x1 163 us: sums(): pl.pallas_call(functools.partial(sum_kernel, count), out_shape=[jax.Shape...]
    psum x1 -> x0, waiting for transfers between devices: 318 us -> none  [step(): summed[number] = [lax.psum(by_w[name], 'dp') for name in NAMES]]
    dot_general x15 -> x0, matrix products: 179 us -> none  [the longest x5 67.3 us: layer(): gate = jnp.dot(a, w['w_gate'], preferred_element_type=jnp.float32)]
    convert_element_type x2 -> x0, other arithmetic: 43.2 us -> none  [adamw(): return ((w - 0.02 * step).astype(jnp.bfloat16), m, v)]
    reduce_sum x4 -> x0, other arithmetic: 12 us -> none  [the longest x3 11.5 us: step(): jnp.sum(g * g)]
  transfers between devices with their start and end apart: 1 -> 0, of which waited for: 1 -> 0; matrix products, arithmetic and copies ran while one was open for 0% -> 0% of each run, Pallas kernels for 0% -> 0%
where the time goes in v2:
time: 342 us
  Pallas kernels  334 us (98%)
  local copies, waits for them, and re-layouts  6.95 us (2%)
    pallas_call x1, Pallas kernels, sums(): pl.pallas_call(functools.partial(sum_kernel, count), out_shape=[jax.Shape...  163 us
    pallas_call x1, Pallas kernels, gradients(): pl.pallas_call(gradients_kernel, out_shape=[jax.ShapeDtypeStruct(s, jnp.b...  121 us
    pallas_call x1, Pallas kernels, adamw(): pl.pallas_call(adamw_kernel, grid=(weights[0].shape[0], steps), out_shape...  50.4 us
    unnamed x10, local copies, waits for them, and re-layouts  6.95 us

profile of v2, /device:TPU:2, one launch (start us, length us, event | category | flops | bytes accessed | tf_op | source)
XLA Modules:
  0.0 341.6 jit_solution(10443304353689590341)
XLA Ops:
  0.6 121.0 %gradients.1 = (bf16[512,2048]{1,0:T(8,128)(2,1)}, bf16[512,2048]{1,0:T(8,128)(2,1)}, bf16[2048,512]{1,0:T(8,128)(2,1)}, bf16[512,2048]{1,0:T(8,128)(2,1)}, bf16...) custom-call(bf16[2048,512]{1,0:T(8,128)(2,1)} %bitcast.18, bf16[2048,512]{1,0:T(8,128)(2,1)} %bitcast.19, ...), custom_call_target="tpu_custom_call" | custom-call | flops 73014444032 | bytes 31457280 | tf_op jit(solution)/shard_map/gradients/pallas_call | solution.py:118
  121.7 0.0 copy-start.1
  121.7 1.6 copy-done.1
  123.3 0.0 copy-start.2
  123.3 1.6 copy-done.2
  124.9 0.0 copy-start.3
  124.9 1.6 copy-done.3
  126.4 0.0 copy-start.4
  126.4 1.6 copy-done.4
  128.0 162.6 %sums.1 = (bf16[2,4,4,2,16,2048]{5,4,3,2,1,0:T(8,128)(2,1)}, bf16[2,4,4,2,16,2048]{5,4,3,2,1,0:T(8,128)(2,1)}, bf16[2,4,4,8,16,512]{5,4,3,2,1,0:T(8,128)(2,1)}, f32[8,128]{1,0:T(8,128)S(1)}) custom-call(bf16[4,4,2,16,2048]{4,3,2,1,0:T(8,128)(2,1)S(1)} %bitcast.11, bf16[4,4,2,16,2048]{4,3,2,1,0:T(8,128)(2,1)S(1)} %bitcast.12, ...), custom_call_target="tpu_custom_call" | custom-call | flops 99999997952 | bytes 25165824 | tf_op jit(solution)/shard_map/sums/pallas_call | solution.py:337
  290.7 0.0 copy-start
  290.7 0.6 copy-done
  291.3 50.4 %adamw.1 = (bf16[2,512,2048]{2,1,0:T(8,128)(2,1)}, f32[2,512,2048]{2,1,0:T(8,128)}, f32[2,512,2048]{2,1,0:T(8,128)}, bf16[2,512,2048]{2,1,0:T(8,128)(2,1)}, f32[...) custom-call(f32[8,128]{1,0:T(8,128)} %copy-done, ...), custom_call_target="tpu_custom_call" | custom-call | flops 100663296 | bytes 138412032 | tf_op jit(solution)/shard_map/adamw/pallas_call | solution.py:377
Async XLA Ops:
  121.7 1.6 copy-start.1
  123.3 1.6 copy-start.2
  124.9 1.6 copy-start.3
  126.4 1.6 copy-start.4
  290.7 0.6 copy-start

commit v3 on v2

v3 whole, which is shorter than its diff:
```python
import functools
import heapq

import jax
import jax.numpy as jnp
from jax import lax
from jax.experimental import pallas as pl
from jax.experimental.pallas import tpu as pltpu
from jax.sharding import PartitionSpec as P

NAMES = ("w_gate", "w_up", "w_down")
SIZES = {"x": 4, "y": 4, "z": 8}
LANES = 256
TOKENS = 512
HIDDEN = 256
MESH = pl.DeviceIdType.MESH
ORDERS = (("x", "y", "z"), ("y", "z", "x"), ("z", "x", "y"))


def dot(a, b, on=(1, 0)):
    return lax.dot_general(a, b, (((on[0],), (on[1],)), ((), ())), preferred_element_type=jnp.float32)


def position():
    dp = lax.axis_index("dp")
    ny, nz = SIZES["y"], SIZES["z"]
    return {"x": dp // (ny * nz), "y": (dp // nz) % ny, "z": dp % nz}


def along(me, axis, delta):
    at = dict(me)
    at[axis] = (me[axis] + delta + SIZES[axis]) % SIZES[axis]
    return {"dp": (at["x"] * SIZES["y"] + at["y"]) * SIZES["z"] + at["z"]}


def columns_at(base, z=None):
    return pl.ds(base, LANES) if z is None else pl.ds(pl.multiple_of(base + (z % 4) * LANES, LANES), LANES)


def region(fixed, wide, base):
    lead = tuple(fixed.get(axis, slice(None)) for axis in "xy")
    if "z" in fixed:
        return lead + ((fixed["z"] // 4, slice(None), columns_at(base, fixed["z"])) if wide else (fixed["z"], slice(None), columns_at(base)))
    return lead + (slice(None), slice(None), pl.ds(base, 4 * LANES if wide else LANES))


def cut(axes, axis, i, wide):
    lead = (slice(None),) * axes.index(axis)
    if wide and axis == "z":
        return lead + (i // 4, slice(None), columns_at(0, i))
    return lead + (i,)


def shape_of(axes, wide, halves=1):
    if wide and "z" in axes:
        return tuple(SIZES[a] for a in axes if a != "z") + (SIZES["z"] // 4, 16, 4 * halves * LANES)
    return tuple(SIZES[a] for a in axes) + (16, halves * LANES)


def at(index, lead, dims):
    full, rest = list(index) + [slice(None)] * (dims - len(index)), iter(lead)
    return tuple(next(rest) if k < dims - 2 and isinstance(part, slice) else part for k, part in enumerate(full))


def add_into(slot, local, index):
    shape, dims = slot.shape[:-2], len(local.shape)
    total = 1
    for n in shape:
        total *= n

    def body(i, _):
        lead, rest = [], i
        for n in reversed(shape):
            lead.insert(0, rest % n)
            rest = rest // n
        term = local[at(index, lead, dims)].astype(jnp.float32)
        slot[tuple(lead)] = (slot[tuple(lead)].astype(jnp.float32) + term).astype(slot.dtype)
        return 0

    lax.fori_loop(0, total, body, 0)


def sum_one(me, wide, base, order, sign, grad, slots, sends, recvs, out, squares, drain):
    axes, local, near = ("x", "y", "z"), None, 1.0
    numbers = iter(range(1000))

    def send(source, target, to):
        number = next(numbers)
        copy = pltpu.make_async_remote_copy(
            src_ref=source, dst_ref=target, send_sem=sends.at[number], recv_sem=recvs.at[number], device_id=to, device_id_type=MESH
        )
        copy.start()
        drain.append(copy)
        return copy

    for phase in range(2):
        axis = order[phase]
        n, p, buffer = SIZES[axis], me[axis], slots[phase]
        near /= n
        target = along(me, axis, sign)

        def block(i):
            return region({axis: i % n}, wide, base) if local is None else cut(axes, axis, i % n, wide)

        held = grad if local is None else local
        for t in range(n - 1):
            source = held.at[block(p - sign + n)] if t == 0 else buffer.at[t - 1]
            copy = send(source, buffer.at[t], target)
            yield 2.2 + 23.0 * near
            copy.wait_recv()
            add_into(buffer.at[t], held, block(p - sign * (t + 2) + 2 * n))
        local = buffer.at[n - 2]
        axes = tuple(a for a in axes if a != axis)
    axis = order[2]
    n, p, buffer = SIZES[axis], me[axis], slots[2]
    copies = [
        send(local.at[cut(axes, axis, (p + delta) % n, wide)], buffer.at[delta - 1], along(me, axis, delta)) for delta in range(1, n)
    ]
    yield 1.0 + 0.7 * n
    total = local[cut(axes, axis, p, wide)].astype(jnp.float32)
    for delta in range(1, n):
        copies[delta - 1].wait_recv()
        total = total + buffer[delta - 1].astype(jnp.float32)
    total = total.astype(out.dtype)
    mine = region(me, wide, base)
    out[mine] = total
    wide_total = total.astype(jnp.float32)
    wide_total = wide_total * wide_total
    width = squares.shape[-1]
    square = jnp.zeros((8, width), jnp.float32)
    for rows in range(0, 16, 8):
        for columns in range(0, LANES, width):
            square = square + wide_total[rows : rows + 8, columns : columns + width]
    squares[...] = square
    copies = [send(out.at[mine], out.at[mine], along(me, axis, delta)) for delta in range(1, n)]
    yield "reduced"
    yield 1.0 + 0.7 * n
    for copy in copies:
        copy.wait_recv()
    fixed = dict(me)
    for phase in (1, 0):
        fixed.pop(order[phase + 1])
        axis = order[phase]
        n, p = SIZES[axis], me[axis]
        target = along(me, axis, sign)
        for t in range(n - 1):
            part = out.at[region({**fixed, axis: (p - sign * t + n) % n}, wide, base)]
            copy = send(part, part, target)
            yield 2.2 + 23.0 * near
            copy.wait_recv()
        near *= n


def norm_one(me, count, squares, factor, slots, sends, recvs, drain):
    total = squares[0]
    for number in range(1, squares.shape[0]):
        total = total + squares[number]
    copy_number = 0
    for (axis, n), buffer in zip(SIZES.items(), slots, strict=True):
        p = me[axis]
        buffer[p] = total
        copies = []
        for delta in range(1, n):
            copy = pltpu.make_async_remote_copy(
                src_ref=buffer.at[p],
                dst_ref=buffer.at[p],
                send_sem=sends.at[copy_number],
                recv_sem=recvs.at[copy_number],
                device_id=along(me, axis, delta),
                device_id_type=MESH,
            )
            copy.start()
            copies.append(copy)
            copy_number += 1
        yield 1.0 + 0.7 * n
        for copy in copies:
            copy.wait_recv()
        total = buffer[0]
        for i in range(1, n):
            total = total + buffer[i]
        drain += copies
    mean = jnp.sum(total, keepdims=True) / count
    factor[...] = jnp.broadcast_to(jnp.minimum(1.0, 0.5 * lax.rsqrt(mean + 1e-30)), factor.shape)


class Flows:
    def __init__(self, last):
        self.now, self.waiting, self.reduced, self.made, self.last = 0.0, [], 0, 0, last

    def add(self, one):
        heapq.heappush(self.waiting, (self.now + next(one), self.made, one))
        self.made += 1

    def until(self, time):
        while self.waiting and self.waiting[0][0] <= time:
            due, number, one = heapq.heappop(self.waiting)
            self.now = max(self.now, due)
            step = next(one, None)
            if step == "reduced":
                self.reduced += 1
                if self.reduced == 12:
                    self.add(self.last())
                step = next(one)
            if step is not None:
                heapq.heappush(self.waiting, (self.now + step, number, one))
        self.now = max(self.now, time)


def step_kernel(count, x_ref, dy_ref, wg_hbm, wu_hbm, wd_hbm, *refs):
    outs, factor, rest = refs[:3], refs[3], refs[4:]
    a_ref, h_ref, b_ref, hid_ref, dgate_ref, dup_ref, one_ref, two_ref, wg_ref, wu_ref, wd_ref, w_sems, x_sem = rest[:13]
    grads, squares, norm, flow_refs = (rest[13:16], rest[16:19]), rest[19], rest[20:25], rest[25:]
    tokens, d = x_ref.shape
    ff = wg_hbm.shape[2]
    blocks = ff // HIDDEN
    me = position()

    barrier = pltpu.get_barrier_semaphore()
    peers = [(axis, delta) for axis, n in SIZES.items() for delta in range(1, n)]
    for axis, delta in peers:
        pl.semaphore_signal(barrier, inc=1, device_id=along(me, axis, delta), device_id_type=MESH)

    def fetch(number, i, slot):
        f = pl.ds(pl.multiple_of(i * HIDDEN, HIDDEN), HIDDEN)
        return (
            pltpu.make_async_copy(wg_hbm.at[number, :, f], wg_ref.at[slot], w_sems.at[slot, 0]),
            pltpu.make_async_copy(wu_hbm.at[number, :, f], wu_ref.at[slot], w_sems.at[slot, 1]),
            pltpu.make_async_copy(wd_hbm.at[number, f, :], wd_ref.at[slot], w_sems.at[slot, 2]),
        )

    def turn(number, i, after):
        if after is not None:
            later = i + 1
            for copy in fetch(number + (later // blocks) * (after - number), later % blocks, later % 2):
                copy.start()
        for copy in fetch(number, i, i % 2):
            copy.wait()

    def over(n, size, body):
        def at_step(i, _):
            body(pl.ds(pl.multiple_of(i * size, size), size))
            return 0

        lax.fori_loop(0, n // size, at_step, 0)

    def normed(source, target):
        def rows(t):
            wide = source[t, :].astype(jnp.float32)
            target[t, :] = (wide * lax.rsqrt(jnp.mean(wide * wide, -1, keepdims=True) + 1e-6)).astype(jnp.bfloat16)

        over(tokens, min(128, tokens), rows)

    def zero(ref):
        def rows(t):
            ref[t, :] = jnp.zeros((min(128, tokens), d), jnp.float32)

        over(tokens, min(128, tokens), rows)

    take = pltpu.make_async_copy(x_ref, h_ref, x_sem)
    take.start()
    for copy in fetch(0, 0, 0):
        copy.start()
    take.wait()

    normed(h_ref, a_ref)
    zero(one_ref)

    def forward(i, _):
        turn(0, i, 1)
        slot = i % 2

        def rows(t):
            a = a_ref[t, :]
            gate, up = dot(a, wg_ref[slot]), dot(a, wu_ref[slot])
            hidden = (gate * jax.nn.sigmoid(gate) * up).astype(jnp.bfloat16)
            one_ref[t, :] += dot(hidden, wd_ref[slot])

        over(tokens, TOKENS, rows)
        return 0

    lax.fori_loop(0, blocks, forward, 0)

    def add(t):
        h = h_ref[t, :].astype(jnp.float32) + one_ref[t, :].astype(jnp.bfloat16).astype(jnp.float32)
        h_ref[t, :] = h.astype(jnp.bfloat16)

    over(tokens, min(128, tokens), add)

    def backward(number, i, after, more, a_ref, by_ref):
        turn(number, i, after)
        slot = i % 2
        gg, gu, gd = grads[number]

        def rows(t):
            a, by = a_ref[t, :], by_ref[t, :]
            gate, up = dot(a, wg_ref[slot]), dot(a, wu_ref[slot])
            by_hidden = dot(by, wd_ref[slot], (1, 1)).astype(jnp.bfloat16).astype(jnp.float32)
            sigmoid = jax.nn.sigmoid(gate)
            silu = gate * sigmoid
            hid_ref[t, :] = (silu * up).astype(jnp.bfloat16)
            dup = (by_hidden * silu).astype(jnp.bfloat16)
            dgate = (by_hidden * up * (sigmoid + silu * (1.0 - sigmoid))).astype(jnp.bfloat16)
            dgate_ref[t, :] = dgate
            dup_ref[t, :] = dup
            if more:
                one_ref[t, :] += dot(dgate, wg_ref[slot], (1, 1))
                two_ref[t, :] += dot(dup, wu_ref[slot], (1, 1))

        over(tokens, TOKENS, rows)
        x, y, z = SIZES.values()
        f = pl.ds(i * HIDDEN, HIDDEN) if isinstance(i, int) else pl.ds(pl.multiple_of(i * HIDDEN, HIDDEN), HIDDEN)
        pairs = HIDDEN // (16 * z)
        first = i * pairs
        down = dot(hid_ref[...], by_ref[...], (0, 0)).astype(jnp.bfloat16)
        gd[first // y, pl.ds(first % y, pairs)] = down.reshape(pairs, z, 16, d)
        for ref, by_ff in ((gg, dgate_ref), (gu, dup_ref)):
            across = dot(a_ref[...], by_ff[...], (0, 0)).astype(jnp.bfloat16)
            ref[:, :, :, :, f] = across.reshape(x, y, z // 4, 16, HIDDEN)

    normed(h_ref, b_ref)
    zero(one_ref)
    zero(two_ref)

    def last_layer(i, _):
        backward(1, i, 0, True, b_ref, dy_ref)
        return 0

    lax.fori_loop(0, blocks, last_layer, 0)

    drain = []
    flows = Flows(lambda: norm_one(me, count, squares, factor, norm[:3], norm[3], norm[4], drain))

    def start(number):
        for half in range(2):
            for which in range(3):
                place = (number * 2 + half) * 3 + which
                slots, sends, recvs = flow_refs[5 * place : 5 * place + 3], flow_refs[5 * place + 3], flow_refs[5 * place + 4]
                base = half * (4 * LANES if which < 2 else LANES)
                out = outs[which].at[number]
                flows.add(
                    sum_one(
                        me, which < 2, base, ORDERS[which], 1 - 2 * half, grads[number][which], slots, sends, recvs, out, squares.at[place], drain
                    )
                )

    pl.semaphore_wait(barrier, len(peers))
    start(1)

    def by_norm(t):
        wide = h_ref[t, :].astype(jnp.float32)
        by = one_ref[t, :].astype(jnp.bfloat16).astype(jnp.float32) + two_ref[t, :].astype(jnp.bfloat16).astype(jnp.float32)
        by = by.astype(jnp.bfloat16).astype(jnp.float32)
        scale = lax.rsqrt(jnp.mean(wide * wide, -1, keepdims=True) + 1e-6)
        inner = jnp.mean(by * wide, -1, keepdims=True)
        by_h = (by * scale - wide * (inner * scale * scale * scale)).astype(jnp.bfloat16).astype(jnp.float32)
        b_ref[t, :] = (dy_ref[t, :].astype(jnp.float32) + by_h).astype(jnp.bfloat16)

    over(tokens, min(128, tokens), by_norm)
    flows.until(2.0)
    for i in range(blocks):
        backward(0, i, 0 if i + 1 < blocks else None, False, a_ref, b_ref)
        flows.until(2.0 + 3.4 * (i + 1))
    start(0)
    flows.until(1e9)
    for copy in drain:
        copy.wait_send()


def sums(x, dy, w_gate, w_up, w_down):
    tokens, d = x.shape
    layers, _, ff = w_gate.shape
    width = min(128, LANES)
    shapes = [shape_of(("x", "y", "z"), i < 2, 2) for i in range(3)]
    steps = sum(n - 1 for n in SIZES.values())
    scratch = [pltpu.VMEM((tokens, d), jnp.bfloat16)] * 3 + [pltpu.VMEM((tokens, HIDDEN), jnp.bfloat16)] * 3
    scratch += [pltpu.VMEM((tokens, d), jnp.float32)] * 2
    scratch += [pltpu.VMEM((2, d, HIDDEN), jnp.bfloat16)] * 2 + [pltpu.VMEM((2, HIDDEN, d), jnp.bfloat16)]
    scratch += [pltpu.SemaphoreType.DMA((2, 3)), pltpu.SemaphoreType.DMA]
    scratch += [pltpu.VMEM(shape, jnp.bfloat16) for shape in shapes * 2]
    scratch += [pltpu.VMEM((12, 8, width), jnp.float32)] + [pltpu.VMEM((n, 8, width), jnp.float32) for n in SIZES.values()]
    scratch += [pltpu.SemaphoreType.DMA((steps,))] * 2
    for place in range(12):
        which = place % 3
        axes = ("x", "y", "z")
        for phase in range(3):
            axes = tuple(a for a in axes if a != ORDERS[which][phase])
            scratch.append(pltpu.VMEM((SIZES[ORDERS[which][phase]] - 1,) + shape_of(axes, which < 2), jnp.bfloat16))
        scratch += [pltpu.SemaphoreType.DMA((2 * steps,))] * 2
    return pl.pallas_call(
        functools.partial(step_kernel, layers * 3 * d * ff),
        out_shape=[jax.ShapeDtypeStruct((layers,) + shape, jnp.bfloat16) for shape in shapes] + [jax.ShapeDtypeStruct((8, 128), jnp.float32)],
        in_specs=[pl.BlockSpec(memory_space=pl.ANY), pl.BlockSpec(memory_space=pltpu.VMEM)] + [pl.BlockSpec(memory_space=pl.ANY)] * 3,
        out_specs=[pl.BlockSpec(memory_space=pltpu.VMEM)] * 4,
        scratch_shapes=scratch,
        compiler_params=pltpu.CompilerParams(collective_id=0, has_side_effects=True, vmem_limit_bytes=67043328),
        cost_estimate=pl.CostEstimate(flops=34 * tokens * d * ff, bytes_accessed=60 << 20, transcendentals=3 * tokens * ff),
        name="sums",
    )(x, dy, w_gate, w_up, w_down)


def adamw_kernel(factor_ref, *refs):
    factor = factor_ref[0:1, 0:1]
    for k in range(3):
        (g_ref, w_ref, m_ref, v_ref), (w_out, m_out, v_out) = refs[4 * k : 4 * k + 4], refs[12 + 3 * k : 15 + 3 * k]
        rows, columns = w_ref.shape[1:]

        def body(r, _):
            here = (0, pl.ds(pl.multiple_of(r * 16, 16), 16))
            for c in range(0, columns, 512):
                at = here + (pl.ds(c, 512),)
                g = g_ref[at].astype(jnp.float32) * factor
                m = 0.9 * m_ref[at] + 0.1 * g
                v = 0.95 * v_ref[at] + 0.05 * g * g
                w = w_ref[at].astype(jnp.float32)
                step = m * lax.rsqrt(v + 1e-8) + 0.1 * w
                w_out[at] = (w - 0.02 * step).astype(jnp.bfloat16)
                m_out[at] = m
                v_out[at] = v
            return 0

        lax.fori_loop(0, rows // 16, body, 0, unroll=max(1, 512 * 4 // columns))


def adamw(weights, m, v, g, factor, steps=8):
    blocks = [pl.BlockSpec((1, w.shape[1] // steps, w.shape[2]), lambda i, j: (i, j, 0)) for w in weights]
    size = sum(w.size for w in weights)
    shapes = [jax.ShapeDtypeStruct(w.shape, t) for w in weights for t in (jnp.bfloat16, jnp.float32, jnp.float32)]
    out = pl.pallas_call(
        adamw_kernel,
        grid=(weights[0].shape[0], steps),
        out_shape=shapes,
        in_specs=[pl.BlockSpec((8, 128), lambda i, j: (0, 0))] + [block for block in blocks for _ in range(4)],
        out_specs=[block for block in blocks for _ in range(3)],
        compiler_params=pltpu.CompilerParams(vmem_limit_bytes=63 << 20),
        cost_estimate=pl.CostEstimate(flops=16 * size, bytes_accessed=22 * size, transcendentals=size),
        name="adamw",
    )(factor, *(one for four in zip(g, weights, m, v, strict=True) for one in four))
    return [out[3 * k : 3 * k + 3] for k in range(3)]


def solution(mesh):
    def step(x, dy, *arrays):
        weights, m, v = (arrays[i : i + 3] for i in (0, 3, 6))
        *summed, factor = sums(x[0], dy[0], *weights)
        new = adamw(weights, m, v, [s.reshape(w.shape) for s, w in zip(summed, weights, strict=True)], factor)
        return tuple(one[which] for which in range(3) for one in new)

    return jax.shard_map(
        step,
        mesh=mesh,
        in_specs=(P(("rep", "dp"), None, None),) * 2 + (P(None, None, None),) * 9,
        out_specs=(P("rep", None, None),) * 9,
        check_vma=False,
    )
```

time: 342 us -> 314 us (0.918)
  Pallas kernels: 334 us -> 313 us
  local copies, waits for them, and re-layouts: 6.95 us -> 0 us
    pallas_call x2 -> x1, Pallas kernels: 284 us -> 263 us  [sums(): pl.pallas_call(functools.partial(step_kernel, layers * 3 * d * ff), out_s...]
    unnamed x10 -> x0, local copies, waits for them, and re-layouts: 6.95 us -> none
where the time goes in v3:
time: 314 us
  Pallas kernels  313 us (100%)
    pallas_call x1, Pallas kernels, sums(): pl.pallas_call(functools.partial(step_kernel, layers * 3 * d * ff), out_s...  263 us
    pallas_call x1, Pallas kernels, adamw(): pl.pallas_call(adamw_kernel, grid=(weights[0].shape[0], steps), out_shape...  50.4 us

profile of v3, /device:TPU:2, one launch (start us, length us, event | category | flops | bytes accessed | tf_op | source)
XLA Modules:
  0.0 314.0 jit_solution(2238670373499448097)
XLA Ops:
  0.6 262.8 %sums.1 = (bf16[2,4,4,2,16,2048]{5,4,3,2,1,0:T(8,128)(2,1)}, bf16[2,4,4,2,16,2048]{5,4,3,2,1,0:T(8,128)(2,1)}, bf16[2,4,4,8,16,512]{5,4,3,2,1,0:T(8,128)(2,1)}, f32[8,128]{1,0:T(8,128)}) custom-call(bf16[2048,512]{1,0:T(8,128)(2,1)} %bitcast.8, bf16[2048,512]{1,0:T(8,128)(2,1)} %bitcast.9, bf16[2,512,2048]{2,1,0:T(8,128)(2,1)} %refs_1_.1, ...), custom_call_target="tpu_custom_call" | custom-call | flops 73014444032 | bytes 62914560 | tf_op jit(solution)/shard_map/sums/pallas_call | solution.py:389
  263.4 50.4 %adamw.1 = (bf16[2,512,2048]{2,1,0:T(8,128)(2,1)}, f32[2,512,2048]{2,1,0:T(8,128)}, f32[2,512,2048]{2,1,0:T(8,128)}, bf16[2,512,2048]{2,1,0:T(8,128)(2,1)}, f32[...) custom-call(f32[8,128]{1,0:T(8,128)} %get-tuple-element.22.factor_re, ...), custom_call_target="tpu_custom_call" | custom-call | flops 100663296 | bytes 138412032 | tf_op jit(solution)/shard_map/adamw/pallas_call | solution.py:428
